TPU v7x, 64 devices: a 2x2x8 block of a 4x4x8 slice. The times are simulated.
64 devices in a mesh: rep: 4 (over x, y), dp: 16 (over z, core).
Axes of the slice: x: 2, y: 2, z: 8, core: 2. Of those that a mesh axis runs over, the one named last changes fastest.
The devices are a block of a 4x4x8 slice.
Arguments:
- x: bfloat16 [64, 2048, 640], P(('rep', 'dp')), parts along dimension 0
- dy: bfloat16 [64, 2048, 640], P(('rep', 'dp')), parts along dimension 0
- w_gate: bfloat16 [2, 640, 2048], replicated
- w_up: bfloat16 [2, 640, 2048], replicated
- w_down: bfloat16 [2, 2048, 640], replicated
- m_w_gate: float32 [2, 640, 2048], P(None, 'dp')
- m_w_up: float32 [2, 640, 2048], P(None, 'dp')
- m_w_down: float32 [2, 2048, 640], P(None, 'dp')
- v_w_gate: float32 [2, 640, 2048], P(None, 'dp')
- v_w_up: float32 [2, 640, 2048], P(None, 'dp')
- v_w_down: float32 [2, 2048, 640], P(None, 'dp')
Outputs:
- output 1: bfloat16 [8, 640, 2048], P('rep'), parts along dimension 0
- output 2: bfloat16 [8, 640, 2048], P('rep'), parts along dimension 0
- output 3: bfloat16 [8, 2048, 640], P('rep'), parts along dimension 0
- output 4: float32 [8, 640, 2048], P('rep', 'dp'), parts along dimension 0
- output 5: float32 [8, 640, 2048], P('rep', 'dp'), parts along dimension 0
- output 6: float32 [8, 2048, 640], P('rep', 'dp'), parts along dimension 0
- output 7: float32 [8, 640, 2048], P('rep', 'dp'), parts along dimension 0
- output 8: float32 [8, 640, 2048], P('rep', 'dp'), parts along dimension 0
- output 9: float32 [8, 2048, 640], P('rep', 'dp'), parts along dimension 0
There are 4 independent parts. A program takes and returns all parts, laid end to end along the dimension named above; an argument that names none is the same for every part.
All inputs are finite; a program needn't handle non-finite values.
Results may differ from a plain program's by a relative error of at most 0.022.
Values are sent between devices in bfloat16 or wider.
A program may use at most 768 MiB of HBM per device.

v0:
```python
import jax
import jax.numpy as jnp
from jax import lax

NAMES = ("w_gate", "w_up", "w_down")


def matmul(a, w):
    return jnp.dot(a, w, preferred_element_type=jnp.float32).astype(jnp.bfloat16)


def normed(h):
    wide = h.astype(jnp.float32)
    scale = lax.rsqrt(jnp.mean(wide**2, -1, keepdims=True) + 1e-6)
    return (wide * scale).astype(jnp.bfloat16)


def layer(h, w):
    a = normed(h)
    gate = jnp.dot(a, w["w_gate"], preferred_element_type=jnp.float32)
    up = jnp.dot(a, w["w_up"], preferred_element_type=jnp.float32)
    return h + matmul((jax.nn.silu(gate) * up).astype(jnp.bfloat16), w["w_down"])


def adamw(w, m, v, g):
    m = 0.9 * m + 0.1 * g
    v = 0.95 * v + 0.05 * g * g
    step = m * lax.rsqrt(v + 1e-8) + 0.1 * w
    return (w - 0.02 * step).astype(jnp.bfloat16), m, v


def stack(weights, h):
    for number in range(weights["w_gate"].shape[0]):
        h = layer(h, {name: w[number] for name, w in weights.items()})
    return h


def solution(mesh):
    groups = mesh.shape["rep"]

    def step(x, dy, *arrays):
        weights, m, v = (arrays[i : i + 3] for i in (0, 3, 6))
        x, dy = (t.reshape(groups, -1, *t.shape[1:]) for t in (x, dy))

        def of_a_group(x, dy):
            _, back = jax.vjp(lambda w: stack(w, x), dict(zip(NAMES, weights, strict=True)))
            by_weights = back(dy)[0]
            gradients = [by_weights[name].astype(jnp.float32) for name in NAMES]
            new = [adamw(w.astype(jnp.float32), m, v, g) for w, m, v, g in zip(weights, m, v, gradients, strict=True)]
            return tuple(one[which] for which in range(3) for one in new)

        return tuple(t.reshape(-1, *t.shape[2:]) for t in jax.vmap(of_a_group)(x, dy))

    return step
```

profile of v0, /device:TPU:21, one launch (start us, length us, event | category | flops | bytes accessed | tf_op | source)
XLA Modules:
  0.0 827.0 jit_solution(15522357093090734960)
XLA Ops:
  9.7 4.4 copy
  16.8 11.4 %convolution_convert_fusion.1 = bf16[2048,2048]{1,0:T(8,128)(2,1)} fusion(bf16[1,2048,640]{2,1,0:T(8,128)(2,1)} %param.17, bf16[2,2048,640]{2,1,0:T(8,128)(2,1)} %param.16), kind=kOutput, calls=%fused_computation.205 | convolution fusion | flops 5372903424 | bytes 13631488 | tf_op jit(solution)/vmap(transpose(jvp()))/dot_general | solution.py:9
  28.1 11.6 %fusion.198 = f32[2048,2048]{1,0:T(8,128)} fusion(bf16[2,640,2048]{2,1,0:T(8,128)(2,1)} %param.12, bf16[1,2048,640]{2,1,0:T(8,128)(2,1)S(1)} %copy-done.15, f32[2048]{0:T(1024)S(1)} %add_rsqrt_fusion), kind=kOutput, calls=%fused_computation.238 | convolution fusion | flops 5372641280 | bytes 22028288 | tf_op jit(solution)/vmap(jvp())/dot_general | solution.py:20
  39.7 18.6 %fusion.156 = (bf16[1,1,2048,2048]{3,2,1,0:T(8,128)(2,1)}, f32[2048,2048]{1,0:T(8,128)}) fusion(f32[2048,2048]{1,0:T(8,128)} %fusion.198, bf16[2,640,2048]{2,1,0:T(8,128)(2,1)} %param.15, bf16[1,2048,640]{2,1,0:T(8,128)(2,1)S(1)} %copy-done.15, f32[2048]{0:T(1024)S(1)} %add_rsqrt_fusion), kind=kOutput, calls=%fused_computation.191 | convolution fusion | flops 5397807104 | bytes 47194112 | tf_op jit(solution)/vmap(jvp())/dot_general | solution.py:21
  58.4 10.0 %fusion.166 = (f32[2048]{0:T(1024)S(1)}, bf16[1,1,2048,640]{2,3,1,0:T(8,128)(2,1)S(1)}) fusion(bf16[2,2048,640]{2,1,0:T(8,128)(2,1)} %param.16, bf16[1,1,2048,2048]{3,2,1,0:T(8,128)(2,1)} %get-tuple-element.263, bf16[1,2048,640]{1,2,0:T(8,128)(2,1)} %copy), kind=kOutput, calls=%fused_computation.213 | convolution fusion | flops 5375260672 | bytes 16261120 | tf_op jit(solution)/vmap(jvp())/dot_general | solution.py:9
  70.5 8.6 %fusion.188 = f32[2048,2048]{1,0:T(8,128)S(1)} fusion(bf16[1,1,2048,640]{2,3,1,0:T(8,128)(2,1)S(1)} %fusion.167, bf16[2,640,2048]{2,1,0:T(8,128)(2,1)} %param.15), kind=kOutput, calls=%fused_computation.228 | convolution fusion | flops 5368709120 | bytes 22020096 | tf_op jit(solution)/vmap(jvp())/dot_general | solution.py:21
  79.2 20.7 %fusion.145 = (bf16[1,1,2048,2048]{3,2,1,0:T(8,128)(2,1)}, bf16[1,1,2048,2048]{3,2,1,0:T(8,128)(2,1)}, f32[2048,2048]{1,0:T(8,128)}) fusion(f32[2048,2048]{1,0:T(8,128)S(1)} %fusion.188, bf16[2048,2048]{1,0:T(8,128)(2,1)} %convolution_convert_fusion.1, bf16[2,640,2048]{2,1,0:T(8,128)(2,1)} %param.12, bf16[1,1,2048,640]{2,3,1,0:T(8,128)(2,1)S(1)} %fusion.167), kind=kOutput, calls=%fused_computation.175 | convolution fusion | flops 5431623680 | bytes 63963136 | tf_op jit(solution)/vmap(jvp())/dot_general | solution.py:20
  99.9 11.1 %fusion.155 = bf16[1,1,2048,2048]{3,2,1,0:T(8,128)(2,1)} fusion(f32[2048,2048]{1,0:T(8,128)S(1)} %fusion.188, f32[2048,2048]{1,0:T(8,128)} %get-tuple-element.267), kind=kLoop, calls=%fused_computation.189 | loop fusion | flops 25165824 | bytes 41943040 | tf_op jit(solution)/vmap(jvp())/convert_element_type | solution.py:22
  111.0 12.5 %copy.2 = bf16[1,1,2048,2048]{2,3,1,0:T(8,128)(2,1)} copy(bf16[1,1,2048,2048]{3,2,1,0:T(8,128)(2,1)} %fusion.155) | data formatting | bytes 16777216
  123.6 4.5 copy.3
  128.0 84.2 %while.16 = (bf16[1,1,2048,2048]{2,3,1,0:T(8,128)(2,1)}, bf16[1,1,2048,640]{3,2,1,0:T(8,128)(2,1)}, f32[1,128,640]{2,1,0:T(8,128)S(1)}, f32[1,128,640]{2,1,0:T(8...) while((bf16[1,1,2048,2048]{2,3,1,0:T(8,128)(2,1)}, ...), condition=%wide.windowed_dot_general_cond_rs.4.clone, body=%wide.windowed_dot_general_body_rs.4.clone.sunk | while | flops 1346863104 | bytes 77857440 | solution.py:9
  150.5 4.6 collective-permute-start.17
  212.2 12.5 %copy.4 = bf16[1,1,2048,2048]{2,3,1,0:T(8,128)(2,1)} copy(bf16[1,1,2048,2048]{3,2,1,0:T(8,128)(2,1)} %get-tuple-element.263) | data formatting | bytes 16777216
  224.7 9.8 %fusion.172 = bf16[2048,640]{0,1:T(8,128)(2,1)S(1)} fusion(bf16[1,1,2048,2048]{3,2,1,0:T(8,128)(2,1)} %get-tuple-element.622, bf16[2,640,2048]{2,1,0:T(8,128)(2,1)} %param.15), kind=kOutput, calls=%fused_computation.218 | convolution fusion | flops 5368709120 | bytes 13631488 | tf_op jit(solution)/vmap(transpose(jvp()))/dot_general | solution.py:21
  234.5 10.3 %fusion.168 = (f32[2048]{0:T(1024)S(1)}, bf16[2048,640]{0,1:T(8,128)(2,1)S(1)}) fusion(bf16[1,1,2048,640]{2,3,1,0:T(8,128)(2,1)S(1)} %copy-done.14, bf16[2048,640]{0,1:T(8,128)(2,1)S(1)} %fusion.172, bf16[2,640,2048]{2,1,0:T(8,128)(2,1)} %param.12, bf16[1,1,2048,2048]{3,2,1,0:T(8,128)(2,1)} %get-tuple-element.544), kind=kOutput, calls=%fused_computation.215 | convolution fusion | flops 5375260672 | bytes 18882560 | tf_op jit(solution)/vmap(transpose(jvp()))/dot_general | solution.py:20
  248.3 4.4 copy.5
  252.7 83.0 %while.17 = (bf16[1,1,2048,2048]{2,3,1,0:T(8,128)(2,1)}, bf16[1,1,2048,640]{3,2,1,0:T(8,128)(2,1)}, f32[1,128,640]{2,1,0:T(8,128)S(1)}, f32[1,128,640]{2,1,0:T(8...) while((bf16[1,1,2048,2048]{2,3,1,0:T(8,128)(2,1)}, ...), condition=%wide.windowed_dot_general_cond_rs.5.clone, body=%wide.windowed_dot_general_body_rs.5.clone.sunk | while | flops 1346863104 | bytes 77857440 | solution.py:9
  336.4 88.9 %while.14 = (bf16[1,1,2048,640]{2,3,1,0:T(8,128)(2,1)S(1)}, bf16[1,1,2048,2048]{3,2,1,0:T(8,128)(2,1)}, f32[1,40,2048]{2,1,0:T(8,128)S(1)}, f32[1,40,2048]{2,1,0...) while((bf16[1,1,2048,640]{2,3,1,0:T(8,128)(2,1)S(1)}, ...), condition=%wide.windowed_dot_general_cond_rs.2.clone, body=%wide.windowed_dot_general_body_rs.2.clone.sunk | while | flops 1343979520 | bytes 58983060 | solution.py:21
  344.0 5.1 fusion.321
  366.4 5.1 fusion.321
  388.9 5.1 fusion.321
  411.4 5.1 fusion.321
  426.0 4.0 multiply_convert_fusion
  430.0 24.5 %convert_multiply_fusion = (bf16[1,1,2048,2048]{3,2,1,0:T(8,128)(2,1)}, bf16[1,1,2048,2048]{3,2,1,0:T(8,128)(2,1)}) fusion(f32[2048,2048]{1,0:T(8,128)} %fusion.198, f32[2048,2048]{1,0:T(8,128)} %get-tuple-element.264, bf16[2,2048,640]{2,1,0:T(8,128)(2,1)} %param.16, bf16[1,1,2048,640]{2,3,1,0:T(8,128)(2,1)} %fusion.181), kind=kOutput, calls=%fused_computation.170 | convolution fusion | flops 5435817984 | bytes 55574528 | tf_op jit(solution)/vmap(transpose(jvp()))/dot_general | solution.py:9
  454.5 92.7 %while.15 = (bf16[1,1,2048,640]{2,3,1,0:T(8,128)(2,1)}, bf16[1,1,2048,2048]{3,2,1,0:T(8,128)(2,1)}, f32[1,40,2048]{2,1,0:T(8,128)S(1)}, f32[1,40,2048]{2,1,0:T(8...) while((bf16[1,1,2048,640]{2,3,1,0:T(8,128)(2,1)}, ...), condition=%wide.windowed_dot_general_cond_rs.3.clone, body=%wide.windowed_dot_general_body_rs.3.clone.sunk | while | flops 1343979520 | bytes 69468848 | solution.py:21
  462.6 5.3 fusion.329
  486.0 5.3 fusion.329
  509.3 5.3 fusion.329
  532.7 5.3 fusion.329
  554.5 97.0 %while.12 = (bf16[1,1,2048,640]{2,3,1,0:T(8,128)(2,1)S(1)}, bf16[1,1,2048,2048]{3,2,1,0:T(8,128)(2,1)}, f32[1,40,2048]{2,1,0:T(8,128)S(1)}, f32[1,40,2048]{2,1,0...) while((bf16[1,1,2048,640]{2,3,1,0:T(8,128)(2,1)S(1)}, ...), condition=%wide.windowed_dot_general_cond_rs.clone, body=%wide.windowed_dot_general_body_rs.clone.sunk | while | flops 1343979520 | bytes 58983060 | solution.py:20
  561.7 5.1 fusion.305
  572.6 4.4 collective-permute-done.2
  576.9 4.8 collective-permute-done.3
  590.8 5.1 fusion.305
  604.3 4.9 collective-permute-done.3
  615.5 5.1 fusion.305
  637.5 5.1 fusion.305
  656.9 98.5 %while.13 = (bf16[1,1,2048,640]{2,3,1,0:T(8,128)(2,1)S(1)}, bf16[1,1,2048,2048]{3,2,1,0:T(8,128)(2,1)}, f32[1,40,2048]{2,1,0:T(8,128)S(1)}, f32[1,40,2048]{2,1,0...) while((bf16[1,1,2048,640]{2,3,1,0:T(8,128)(2,1)S(1)}, ...), condition=%wide.windowed_dot_general_cond_rs.1.clone, body=%wide.windowed_dot_general_body_rs.1.clone.sunk | while | flops 1343979520 | bytes 58983060 | solution.py:20
  664.8 5.1 fusion.313
  679.2 5.3 collective-permute-done.7
  687.8 4.1 collective-permute-start.5
  694.5 5.1 fusion.313
  707.5 4.3 collective-permute-done.7
  718.8 5.1 fusion.313
  741.5 5.1 fusion.313
  756.4 3.9 collective-permute-done.25
  763.4 45.8 %all-gather.10.cloned.1.call-done = bf16[1,2,640,2048]{3,2,1,0:T(8,128)(2,1)} async-done(((bf16[1,2,40,2048]{3,2,1,0:T(8,128)(2,1)}), bf16[1,2,640,2048]{3,2,1,0:T(8,128)(2,1)}) %all-gather.10.cloned.1.call-update) | async-done | bytes 5242896 | tf_op jit(solution)/reshape | solution.py:52
  809.1 6.2 copy.63
  (545 shorter events, 414.7 us)
Async XLA Ops:
  7.2 756.1 %all-gather.14.cloned.1.call-start = ((), (), s32[]{:S(2)}) async-start(), calls=%async_computation.2 | async-start | bytes 5570560 | tf_op jit(solution)/reshape | solution.py:52
  128.0 11.2 %collective-permute-start.16 = (f32[1,128,640]{2,1,0:T(8,128)S(1)}, f32[1,128,640]{2,1,0:T(8,128)}, u32[]{:S(2)}, u32[]{:S(2)}) collective-permute-start(f32[1,128,640]{2,1,0:T(8,128)S(1)} %broadcast_select_fusion.32), channel_id=29, source_target_pairs={{0,1},{1,2},{2,3},{3,4},{4,5},{5,6},{6,7},{7,8},{8,9},{9,10},{10,1... | collective-permute-start | bytes 983048 | tf_op jit(solution)/vmap(transpose(jvp()))/dot_general | solution.py:9
  149.7 11.1 %collective-permute-start.16 = (f32[1,128,640]{2,1,0:T(8,128)S(1)}, f32[1,128,640]{2,1,0:T(8,128)}, u32[]{:S(2)}, u32[]{:S(2)}) collective-permute-start(f32[1,128,640]{2,1,0:T(8,128)S(1)} %broadcast_select_fusion.32), channel_id=29, source_target_pairs={{0,1},{1,2},{2,3},{3,4},{4,5},{5,6},{6,7},{7,8},{8,9},{9,10},{10,1... | collective-permute-start | bytes 983048 | tf_op jit(solution)/vmap(transpose(jvp()))/dot_general | solution.py:9
  150.5 10.3 %collective-permute-start.17 = (f32[1,128,640]{2,1,0:T(8,128)}, f32[1,128,640]{2,1,0:T(8,128)S(1)}, u32[]{:S(2)}, u32[]{:S(2)}) collective-permute-start(f32[1,128,640]{2,1,0:T(8,128)} %broadcast_select_fusion.33), channel_id=28, source_target_pairs={{0,15},{1,0},{2,1},{3,2},{4,3},{5,4},{6,5},{7,6},{8,7},{9,8},{10,9... | collective-permute-start | bytes 983048 | tf_op jit(solution)/vmap(transpose(jvp()))/dot_general | solution.py:9
  171.4 10.4 %collective-permute-start.16 = (f32[1,128,640]{2,1,0:T(8,128)S(1)}, f32[1,128,640]{2,1,0:T(8,128)}, u32[]{:S(2)}, u32[]{:S(2)}) collective-permute-start(f32[1,128,640]{2,1,0:T(8,128)S(1)} %broadcast_select_fusion.32), channel_id=29, source_target_pairs={{0,1},{1,2},{2,3},{3,4},{4,5},{5,6},{6,7},{7,8},{8,9},{9,10},{10,1... | collective-permute-start | bytes 983048 | tf_op jit(solution)/vmap(transpose(jvp()))/dot_general | solution.py:9
  192.3 10.4 %collective-permute-start.16 = (f32[1,128,640]{2,1,0:T(8,128)S(1)}, f32[1,128,640]{2,1,0:T(8,128)}, u32[]{:S(2)}, u32[]{:S(2)}) collective-permute-start(f32[1,128,640]{2,1,0:T(8,128)S(1)} %broadcast_select_fusion.32), channel_id=29, source_target_pairs={{0,1},{1,2},{2,3},{3,4},{4,5},{5,6},{6,7},{7,8},{8,9},{9,10},{10,1... | collective-permute-start | bytes 983048 | tf_op jit(solution)/vmap(transpose(jvp()))/dot_general | solution.py:9
  212.2 337.1 %collective-permute-start.28 = (f32[1,128,640]{2,1,0:T(8,128)}, f32[1,128,640]{2,1,0:T(8,128)}, u32[]{:S(2)}, u32[]{:S(2)}) collective-permute-start(f32[1,128,640]{2,1,0:T(8,128)} %get-tuple-element.45), channel_id=32, source_target_pairs={{0,1},{1,2},{2,3},{3,4},{4,5},{5,6},{6,7},{7,8},{8,9},{9,10},{10,1... | collective-permute-start | bytes 983048 | tf_op jit(solution)/vmap(transpose(jvp()))/dot_general | solution.py:9
  252.9 10.4 %collective-permute-start.20 = (f32[1,128,640]{2,1,0:T(8,128)S(1)}, f32[1,128,640]{2,1,0:T(8,128)}, u32[]{:S(2)}, u32[]{:S(2)}) collective-permute-start(f32[1,128,640]{2,1,0:T(8,128)S(1)} %broadcast_select_fusion.34), channel_id=35, source_target_pairs={{0,1},{1,2},{2,3},{3,4},{4,5},{5,6},{6,7},{7,8},{8,9},{9,10},{10,1... | collective-permute-start | bytes 983048 | tf_op jit(solution)/vmap(transpose(jvp()))/dot_general | solution.py:9
  273.8 10.4 %collective-permute-start.20 = (f32[1,128,640]{2,1,0:T(8,128)S(1)}, f32[1,128,640]{2,1,0:T(8,128)}, u32[]{:S(2)}, u32[]{:S(2)}) collective-permute-start(f32[1,128,640]{2,1,0:T(8,128)S(1)} %broadcast_select_fusion.34), channel_id=35, source_target_pairs={{0,1},{1,2},{2,3},{3,4},{4,5},{5,6},{6,7},{7,8},{8,9},{9,10},{10,1... | collective-permute-start | bytes 983048 | tf_op jit(solution)/vmap(transpose(jvp()))/dot_general | solution.py:9
  294.8 10.4 %collective-permute-start.20 = (f32[1,128,640]{2,1,0:T(8,128)S(1)}, f32[1,128,640]{2,1,0:T(8,128)}, u32[]{:S(2)}, u32[]{:S(2)}) collective-permute-start(f32[1,128,640]{2,1,0:T(8,128)S(1)} %broadcast_select_fusion.34), channel_id=35, source_target_pairs={{0,1},{1,2},{2,3},{3,4},{4,5},{5,6},{6,7},{7,8},{8,9},{9,10},{10,1... | collective-permute-start | bytes 983048 | tf_op jit(solution)/vmap(transpose(jvp()))/dot_general | solution.py:9
  315.7 10.4 %collective-permute-start.20 = (f32[1,128,640]{2,1,0:T(8,128)S(1)}, f32[1,128,640]{2,1,0:T(8,128)}, u32[]{:S(2)}, u32[]{:S(2)}) collective-permute-start(f32[1,128,640]{2,1,0:T(8,128)S(1)} %broadcast_select_fusion.34), channel_id=35, source_target_pairs={{0,1},{1,2},{2,3},{3,4},{4,5},{5,6},{6,7},{7,8},{8,9},{9,10},{10,1... | collective-permute-start | bytes 983048 | tf_op jit(solution)/vmap(transpose(jvp()))/dot_general | solution.py:9
  335.6 214.7 %collective-permute-start.29 = (f32[1,128,640]{2,1,0:T(8,128)}, f32[1,128,640]{2,1,0:T(8,128)}, u32[]{:S(2)}, u32[]{:S(2)}) collective-permute-start(f32[1,128,640]{2,1,0:T(8,128)} %get-tuple-element.47), channel_id=38, source_target_pairs={{0,1},{1,2},{2,3},{3,4},{4,5},{5,6},{6,7},{7,8},{8,9},{9,10},{10,1... | collective-permute-start | bytes 983048 | tf_op jit(solution)/vmap(transpose(jvp()))/dot_general | solution.py:9
  337.1 12.0 %collective-permute-start.8 = (f32[1,40,2048]{2,1,0:T(8,128)}, f32[1,40,2048]{2,1,0:T(8,128)}, u32[]{:S(2)}, u32[]{:S(2)}) collective-permute-start(f32[1,40,2048]{2,1,0:T(8,128)} %broadcast_select_fusion.28), channel_id=16, source_target_pairs={{0,1},{1,2},{2,3},{3,4},{4,5},{5,6},{6,7},{7,8},{8,9},{9,10},{10,1... | collective-permute-start | bytes 983048 | tf_op jit(solution)/vmap(transpose(jvp()))/dot_general | solution.py:21
  339.0 10.1 %collective-permute-start.9 = (f32[1,40,2048]{2,1,0:T(8,128)}, f32[1,40,2048]{2,1,0:T(8,128)S(1)}, u32[]{:S(2)}, u32[]{:S(2)}) collective-permute-start(f32[1,40,2048]{2,1,0:T(8,128)} %broadcast_select_fusion.29), channel_id=15, source_target_pairs={{0,15},{1,0},{2,1},{3,2},{4,3},{5,4},{6,5},{7,6},{8,7},{9,8},{10,9... | collective-permute-start | bytes 983048 | tf_op jit(solution)/vmap(transpose(jvp()))/dot_general | solution.py:21
  359.6 12.0 %collective-permute-start.8 = (f32[1,40,2048]{2,1,0:T(8,128)}, f32[1,40,2048]{2,1,0:T(8,128)}, u32[]{:S(2)}, u32[]{:S(2)}) collective-permute-start(f32[1,40,2048]{2,1,0:T(8,128)} %broadcast_select_fusion.28), channel_id=16, source_target_pairs={{0,1},{1,2},{2,3},{3,4},{4,5},{5,6},{6,7},{7,8},{8,9},{9,10},{10,1... | collective-permute-start | bytes 983048 | tf_op jit(solution)/vmap(transpose(jvp()))/dot_general | solution.py:21
  360.3 11.2 %collective-permute-start.9 = (f32[1,40,2048]{2,1,0:T(8,128)}, f32[1,40,2048]{2,1,0:T(8,128)S(1)}, u32[]{:S(2)}, u32[]{:S(2)}) collective-permute-start(f32[1,40,2048]{2,1,0:T(8,128)} %broadcast_select_fusion.29), channel_id=15, source_target_pairs={{0,15},{1,0},{2,1},{3,2},{4,3},{5,4},{6,5},{7,6},{8,7},{9,8},{10,9... | collective-permute-start | bytes 983048 | tf_op jit(solution)/vmap(transpose(jvp()))/dot_general | solution.py:21
  382.0 12.0 %collective-permute-start.8 = (f32[1,40,2048]{2,1,0:T(8,128)}, f32[1,40,2048]{2,1,0:T(8,128)}, u32[]{:S(2)}, u32[]{:S(2)}) collective-permute-start(f32[1,40,2048]{2,1,0:T(8,128)} %broadcast_select_fusion.28), channel_id=16, source_target_pairs={{0,1},{1,2},{2,3},{3,4},{4,5},{5,6},{6,7},{7,8},{8,9},{9,10},{10,1... | collective-permute-start | bytes 983048 | tf_op jit(solution)/vmap(transpose(jvp()))/dot_general | solution.py:21
  382.8 11.2 %collective-permute-start.9 = (f32[1,40,2048]{2,1,0:T(8,128)}, f32[1,40,2048]{2,1,0:T(8,128)S(1)}, u32[]{:S(2)}, u32[]{:S(2)}) collective-permute-start(f32[1,40,2048]{2,1,0:T(8,128)} %broadcast_select_fusion.29), channel_id=15, source_target_pairs={{0,15},{1,0},{2,1},{3,2},{4,3},{5,4},{6,5},{7,6},{8,7},{9,8},{10,9... | collective-permute-start | bytes 983048 | tf_op jit(solution)/vmap(transpose(jvp()))/dot_general | solution.py:21
  404.5 12.0 %collective-permute-start.8 = (f32[1,40,2048]{2,1,0:T(8,128)}, f32[1,40,2048]{2,1,0:T(8,128)}, u32[]{:S(2)}, u32[]{:S(2)}) collective-permute-start(f32[1,40,2048]{2,1,0:T(8,128)} %broadcast_select_fusion.28), channel_id=16, source_target_pairs={{0,1},{1,2},{2,3},{3,4},{4,5},{5,6},{6,7},{7,8},{8,9},{9,10},{10,1... | collective-permute-start | bytes 983048 | tf_op jit(solution)/vmap(transpose(jvp()))/dot_general | solution.py:21
  405.3 11.2 %collective-permute-start.9 = (f32[1,40,2048]{2,1,0:T(8,128)}, f32[1,40,2048]{2,1,0:T(8,128)S(1)}, u32[]{:S(2)}, u32[]{:S(2)}) collective-permute-start(f32[1,40,2048]{2,1,0:T(8,128)} %broadcast_select_fusion.29), channel_id=15, source_target_pairs={{0,15},{1,0},{2,1},{3,2},{4,3},{5,4},{6,5},{7,6},{8,7},{9,8},{10,9... | collective-permute-start | bytes 983048 | tf_op jit(solution)/vmap(transpose(jvp()))/dot_general | solution.py:21
  425.3 226.2 %collective-permute-start.26 = (f32[1,40,2048]{2,1,0:T(8,128)}, f32[1,40,2048]{2,1,0:T(8,128)}, u32[]{:S(2)}, u32[]{:S(2)}) collective-permute-start(f32[1,40,2048]{2,1,0:T(8,128)} %get-tuple-element.41), channel_id=19, source_target_pairs={{0,1},{1,2},{2,3},{3,4},{4,5},{5,6},{6,7},{7,8},{8,9},{9,10},{10,1... | collective-permute-start | bytes 983048 | tf_op jit(solution)/vmap(transpose(jvp()))/dot_general | solution.py:21
  455.5 12.4 %collective-permute-start.12 = (f32[1,40,2048]{2,1,0:T(8,128)}, f32[1,40,2048]{2,1,0:T(8,128)}, u32[]{:S(2)}, u32[]{:S(2)}) collective-permute-start(f32[1,40,2048]{2,1,0:T(8,128)} %broadcast_select_fusion.30), channel_id=22, source_target_pairs={{0,1},{1,2},{2,3},{3,4},{4,5},{5,6},{6,7},{7,8},{8,9},{9,10},{10,1... | collective-permute-start | bytes 983048 | tf_op jit(solution)/vmap(transpose(jvp()))/dot_general | solution.py:21
  456.8 11.1 %collective-permute-start.13 = (f32[1,40,2048]{2,1,0:T(8,128)}, f32[1,40,2048]{2,1,0:T(8,128)S(1)}, u32[]{:S(2)}, u32[]{:S(2)}) collective-permute-start(f32[1,40,2048]{2,1,0:T(8,128)} %broadcast_select_fusion.31), channel_id=21, source_target_pairs={{0,15},{1,0},{2,1},{3,2},{4,3},{5,4},{6,5},{7,6},{8,7},{9,8},{10,9... | collective-permute-start | bytes 983048 | tf_op jit(solution)/vmap(transpose(jvp()))/dot_general | solution.py:21
  478.9 12.4 %collective-permute-start.12 = (f32[1,40,2048]{2,1,0:T(8,128)}, f32[1,40,2048]{2,1,0:T(8,128)}, u32[]{:S(2)}, u32[]{:S(2)}) collective-permute-start(f32[1,40,2048]{2,1,0:T(8,128)} %broadcast_select_fusion.30), channel_id=22, source_target_pairs={{0,1},{1,2},{2,3},{3,4},{4,5},{5,6},{6,7},{7,8},{8,9},{9,10},{10,1... | collective-permute-start | bytes 983048 | tf_op jit(solution)/vmap(transpose(jvp()))/dot_general | solution.py:21
  479.6 11.7 %collective-permute-start.13 = (f32[1,40,2048]{2,1,0:T(8,128)}, f32[1,40,2048]{2,1,0:T(8,128)S(1)}, u32[]{:S(2)}, u32[]{:S(2)}) collective-permute-start(f32[1,40,2048]{2,1,0:T(8,128)} %broadcast_select_fusion.31), channel_id=21, source_target_pairs={{0,15},{1,0},{2,1},{3,2},{4,3},{5,4},{6,5},{7,6},{8,7},{9,8},{10,9... | collective-permute-start | bytes 983048 | tf_op jit(solution)/vmap(transpose(jvp()))/dot_general | solution.py:21
  502.2 12.4 %collective-permute-start.12 = (f32[1,40,2048]{2,1,0:T(8,128)}, f32[1,40,2048]{2,1,0:T(8,128)}, u32[]{:S(2)}, u32[]{:S(2)}) collective-permute-start(f32[1,40,2048]{2,1,0:T(8,128)} %broadcast_select_fusion.30), channel_id=22, source_target_pairs={{0,1},{1,2},{2,3},{3,4},{4,5},{5,6},{6,7},{7,8},{8,9},{9,10},{10,1... | collective-permute-start | bytes 983048 | tf_op jit(solution)/vmap(transpose(jvp()))/dot_general | solution.py:21
  503.0 11.7 %collective-permute-start.13 = (f32[1,40,2048]{2,1,0:T(8,128)}, f32[1,40,2048]{2,1,0:T(8,128)S(1)}, u32[]{:S(2)}, u32[]{:S(2)}) collective-permute-start(f32[1,40,2048]{2,1,0:T(8,128)} %broadcast_select_fusion.31), channel_id=21, source_target_pairs={{0,15},{1,0},{2,1},{3,2},{4,3},{5,4},{6,5},{7,6},{8,7},{9,8},{10,9... | collective-permute-start | bytes 983048 | tf_op jit(solution)/vmap(transpose(jvp()))/dot_general | solution.py:21
  525.6 12.4 %collective-permute-start.12 = (f32[1,40,2048]{2,1,0:T(8,128)}, f32[1,40,2048]{2,1,0:T(8,128)}, u32[]{:S(2)}, u32[]{:S(2)}) collective-permute-start(f32[1,40,2048]{2,1,0:T(8,128)} %broadcast_select_fusion.30), channel_id=22, source_target_pairs={{0,1},{1,2},{2,3},{3,4},{4,5},{5,6},{6,7},{7,8},{8,9},{9,10},{10,1... | collective-permute-start | bytes 983048 | tf_op jit(solution)/vmap(transpose(jvp()))/dot_general | solution.py:21
  526.3 11.7 %collective-permute-start.13 = (f32[1,40,2048]{2,1,0:T(8,128)}, f32[1,40,2048]{2,1,0:T(8,128)S(1)}, u32[]{:S(2)}, u32[]{:S(2)}) collective-permute-start(f32[1,40,2048]{2,1,0:T(8,128)} %broadcast_select_fusion.31), channel_id=21, source_target_pairs={{0,15},{1,0},{2,1},{3,2},{4,3},{5,4},{6,5},{7,6},{8,7},{9,8},{10,9... | collective-permute-start | bytes 983048 | tf_op jit(solution)/vmap(transpose(jvp()))/dot_general | solution.py:21
  547.2 105.5 %collective-permute-start.27 = (f32[1,40,2048]{2,1,0:T(8,128)}, f32[1,40,2048]{2,1,0:T(8,128)}, u32[]{:S(2)}, u32[]{:S(2)}) collective-permute-start(f32[1,40,2048]{2,1,0:T(8,128)} %get-tuple-element.43), channel_id=25, source_target_pairs={{0,1},{1,2},{2,3},{3,4},{4,5},{5,6},{6,7},{7,8},{8,9},{9,10},{10,1... | collective-permute-start | bytes 983048 | tf_op jit(solution)/vmap(transpose(jvp()))/dot_general | solution.py:21
  554.4 209.0 %all-gather.12.cloned.1.call-start = ((), (), s32[]{:S(2)}) async-start(), calls=%async_computation.1 | async-start | bytes 5570560 | tf_op jit(solution)/reshape | solution.py:52
  554.5 12.3 %collective-permute-start = (f32[1,40,2048]{2,1,0:T(8,128)S(1)}, f32[1,40,2048]{2,1,0:T(8,128)}, u32[]{:S(2)}, u32[]{:S(2)}) collective-permute-start(f32[1,40,2048]{2,1,0:T(8,128)S(1)} %broadcast_select_fusion.24), channel_id=3, source_target_pairs={{0,1},{1,2},{2,3},{3,4},{4,5},{5,6},{6,7},{7,8},{8,9},{9,10},{10,1... | collective-permute-start | bytes 983048 | tf_op jit(solution)/vmap(transpose(jvp()))/dot_general | solution.py:20
  555.9 11.0 %collective-permute-start.1 = (f32[1,40,2048]{2,1,0:T(8,128)}, f32[1,40,2048]{2,1,0:T(8,128)S(1)}, u32[]{:S(2)}, u32[]{:S(2)}) collective-permute-start(f32[1,40,2048]{2,1,0:T(8,128)} %broadcast_select_fusion.25), channel_id=2, source_target_pairs={{0,15},{1,0},{2,1},{3,2},{4,3},{5,4},{6,5},{7,6},{8,7},{9,8},{10,9... | collective-permute-start | bytes 983048 | tf_op jit(solution)/vmap(transpose(jvp()))/dot_general | solution.py:20
  568.0 13.8 %collective-permute-start.3 = (f32[1,40,2048]{2,1,0:T(8,128)S(1)}, f32[1,40,2048]{2,1,0:T(8,128)S(1)}, u32[]{:S(2)}, u32[]{:S(2)}) collective-permute-start(f32[1,40,2048]{2,1,0:T(8,128)S(1)} %get-tuple-element.456), channel_id=4, source_target_pairs={{0,15},{1,0},{2,1},{3,2},{4,3},{5,4},{6,5},{7,6},{8,7},{9,8},{10,9... | collective-permute-start | bytes 983048 | tf_op jit(solution)/vmap(transpose(jvp()))/dot_general | solution.py:20
  583.6 12.4 %collective-permute-start = (f32[1,40,2048]{2,1,0:T(8,128)S(1)}, f32[1,40,2048]{2,1,0:T(8,128)}, u32[]{:S(2)}, u32[]{:S(2)}) collective-permute-start(f32[1,40,2048]{2,1,0:T(8,128)S(1)} %broadcast_select_fusion.24), channel_id=3, source_target_pairs={{0,1},{1,2},{2,3},{3,4},{4,5},{5,6},{6,7},{7,8},{8,9},{9,10},{10,1... | collective-permute-start | bytes 983048 | tf_op jit(solution)/vmap(transpose(jvp()))/dot_general | solution.py:20
  584.4 14.0 %collective-permute-start.1 = (f32[1,40,2048]{2,1,0:T(8,128)}, f32[1,40,2048]{2,1,0:T(8,128)S(1)}, u32[]{:S(2)}, u32[]{:S(2)}) collective-permute-start(f32[1,40,2048]{2,1,0:T(8,128)} %broadcast_select_fusion.25), channel_id=2, source_target_pairs={{0,15},{1,0},{2,1},{3,2},{4,3},{5,4},{6,5},{7,6},{8,7},{9,8},{10,9... | collective-permute-start | bytes 983048 | tf_op jit(solution)/vmap(transpose(jvp()))/dot_general | solution.py:20
  610.9 9.6 %collective-permute-start = (f32[1,40,2048]{2,1,0:T(8,128)S(1)}, f32[1,40,2048]{2,1,0:T(8,128)}, u32[]{:S(2)}, u32[]{:S(2)}) collective-permute-start(f32[1,40,2048]{2,1,0:T(8,128)S(1)} %broadcast_select_fusion.24), channel_id=3, source_target_pairs={{0,1},{1,2},{2,3},{3,4},{4,5},{5,6},{6,7},{7,8},{8,9},{9,10},{10,1... | collective-permute-start | bytes 983048 | tf_op jit(solution)/vmap(transpose(jvp()))/dot_general | solution.py:20
  630.9 11.8 %collective-permute-start = (f32[1,40,2048]{2,1,0:T(8,128)S(1)}, f32[1,40,2048]{2,1,0:T(8,128)}, u32[]{:S(2)}, u32[]{:S(2)}) collective-permute-start(f32[1,40,2048]{2,1,0:T(8,128)S(1)} %broadcast_select_fusion.24), channel_id=3, source_target_pairs={{0,1},{1,2},{2,3},{3,4},{4,5},{5,6},{6,7},{7,8},{8,9},{9,10},{10,1... | collective-permute-start | bytes 983048 | tf_op jit(solution)/vmap(transpose(jvp()))/dot_general | solution.py:20
  631.7 10.9 %collective-permute-start.1 = (f32[1,40,2048]{2,1,0:T(8,128)}, f32[1,40,2048]{2,1,0:T(8,128)S(1)}, u32[]{:S(2)}, u32[]{:S(2)}) collective-permute-start(f32[1,40,2048]{2,1,0:T(8,128)} %broadcast_select_fusion.25), channel_id=2, source_target_pairs={{0,15},{1,0},{2,1},{3,2},{4,3},{5,4},{6,5},{7,6},{8,7},{9,8},{10,9... | collective-permute-start | bytes 983048 | tf_op jit(solution)/vmap(transpose(jvp()))/dot_general | solution.py:20
  651.4 104.0 %collective-permute-start.24 = (f32[1,40,2048]{2,1,0:T(8,128)}, f32[1,40,2048]{2,1,0:T(8,128)}, u32[]{:S(2)}, u32[]{:S(2)}) collective-permute-start(f32[1,40,2048]{2,1,0:T(8,128)} %get-tuple-element.37), channel_id=6, source_target_pairs={{0,1},{1,2},{2,3},{3,4},{4,5},{5,6},{6,7},{7,8},{8,9},{9,10},{10,1... | collective-permute-start | bytes 983048 | tf_op jit(solution)/vmap(transpose(jvp()))/dot_general | solution.py:20
  656.8 152.4 %all-gather.10.cloned.1.call-start = ((), (), s32[]{:S(2)}) async-start(), calls=%async_computation | async-start | bytes 5570560 | tf_op jit(solution)/reshape | solution.py:52
  657.6 12.2 %collective-permute-start.4 = (f32[1,40,2048]{2,1,0:T(8,128)}, f32[1,40,2048]{2,1,0:T(8,128)}, u32[]{:S(2)}, u32[]{:S(2)}) collective-permute-start(f32[1,40,2048]{2,1,0:T(8,128)} %broadcast_select_fusion.26), channel_id=9, source_target_pairs={{0,1},{1,2},{2,3},{3,4},{4,5},{5,6},{6,7},{7,8},{8,9},{9,10},{10,1... | collective-permute-start | bytes 983048 | tf_op jit(solution)/vmap(transpose(jvp()))/dot_general | solution.py:20
  659.0 10.9 %collective-permute-start.5 = (f32[1,40,2048]{2,1,0:T(8,128)}, f32[1,40,2048]{2,1,0:T(8,128)S(1)}, u32[]{:S(2)}, u32[]{:S(2)}) collective-permute-start(f32[1,40,2048]{2,1,0:T(8,128)} %broadcast_select_fusion.27), channel_id=8, source_target_pairs={{0,15},{1,0},{2,1},{3,2},{4,3},{5,4},{6,5},{7,6},{8,7},{9,8},{10,9... | collective-permute-start | bytes 983048 | tf_op jit(solution)/vmap(transpose(jvp()))/dot_general | solution.py:20
  671.0 13.5 %collective-permute-start.7 = (f32[1,40,2048]{2,1,0:T(8,128)S(1)}, f32[1,40,2048]{2,1,0:T(8,128)S(1)}, u32[]{:S(2)}, u32[]{:S(2)}) collective-permute-start(f32[1,40,2048]{2,1,0:T(8,128)S(1)} %get-tuple-element.465), channel_id=10, source_target_pairs={{0,15},{1,0},{2,1},{3,2},{4,3},{5,4},{6,5},{7,6},{8,7},{9,8},{10,9... | collective-permute-start | bytes 983048 | tf_op jit(solution)/vmap(transpose(jvp()))/dot_general | solution.py:20
  687.1 12.5 %collective-permute-start.4 = (f32[1,40,2048]{2,1,0:T(8,128)}, f32[1,40,2048]{2,1,0:T(8,128)}, u32[]{:S(2)}, u32[]{:S(2)}) collective-permute-start(f32[1,40,2048]{2,1,0:T(8,128)} %broadcast_select_fusion.26), channel_id=9, source_target_pairs={{0,1},{1,2},{2,3},{3,4},{4,5},{5,6},{6,7},{7,8},{8,9},{9,10},{10,1... | collective-permute-start | bytes 983048 | tf_op jit(solution)/vmap(transpose(jvp()))/dot_general | solution.py:20
  687.8 14.5 %collective-permute-start.5 = (f32[1,40,2048]{2,1,0:T(8,128)}, f32[1,40,2048]{2,1,0:T(8,128)S(1)}, u32[]{:S(2)}, u32[]{:S(2)}) collective-permute-start(f32[1,40,2048]{2,1,0:T(8,128)} %broadcast_select_fusion.27), channel_id=8, source_target_pairs={{0,15},{1,0},{2,1},{3,2},{4,3},{5,4},{6,5},{7,6},{8,7},{9,8},{10,9... | collective-permute-start | bytes 983048 | tf_op jit(solution)/vmap(transpose(jvp()))/dot_general | solution.py:20
  735.0 11.7 %collective-permute-start.4 = (f32[1,40,2048]{2,1,0:T(8,128)}, f32[1,40,2048]{2,1,0:T(8,128)}, u32[]{:S(2)}, u32[]{:S(2)}) collective-permute-start(f32[1,40,2048]{2,1,0:T(8,128)} %broadcast_select_fusion.26), channel_id=9, source_target_pairs={{0,1},{1,2},{2,3},{3,4},{4,5},{5,6},{6,7},{7,8},{8,9},{9,10},{10,1... | collective-permute-start | bytes 983048 | tf_op jit(solution)/vmap(transpose(jvp()))/dot_general | solution.py:20
  735.7 10.9 %collective-permute-start.5 = (f32[1,40,2048]{2,1,0:T(8,128)}, f32[1,40,2048]{2,1,0:T(8,128)S(1)}, u32[]{:S(2)}, u32[]{:S(2)}) collective-permute-start(f32[1,40,2048]{2,1,0:T(8,128)} %broadcast_select_fusion.27), channel_id=8, source_target_pairs={{0,15},{1,0},{2,1},{3,2},{4,3},{5,4},{6,5},{7,6},{8,7},{9,8},{10,9... | collective-permute-start | bytes 983048 | tf_op jit(solution)/vmap(transpose(jvp()))/dot_general | solution.py:20
  (127 other events, 1143.7 us)
Sparse Core Ops, SparseCore 0:
  554.5 49.9 all-gather.13
  656.9 49.0 all-gather.11
  763.4 45.6 all-gather.9
where the time goes:
time: 838 us; the launch traced here: 827 us
  matrix products  267 us (32%)
  starting transfers between devices  161 us (19%)
  other arithmetic  133 us (16%)
  waiting for transfers between devices  133 us (16%)
  local copies, waits for them, and re-layouts  70.2 us (8%)
  loops' own time  47.7 us (6%)
  between operations  15.1 us (2%)
    dot_general x19, matrix products, layer(): gate = jnp.dot(a, w['w_gate'], preferred_element_type=jnp.float32)  96.2 us
    dot_general x19, matrix products, layer(): up = jnp.dot(a, w['w_up'], preferred_element_type=jnp.float32)  91.3 us
    dot_general x19, matrix products, matmul(): jnp.dot(a, w, preferred_element_type=jnp.float32).astype(jnp.bfloat16)  79.3 us
    dot_general x34, starting transfers between devices, matmul(): jnp.dot(a, w, preferred_element_type=jnp.float32).astype(jnp.bfloat16)  57.7 us
    unnamed x45, local copies, waits for them, and re-layouts  55.3 us
    dot_general x34, starting transfers between devices, layer(): up = jnp.dot(a, w['w_up'], preferred_element_type=jnp.float32)  54.9 us
    dot_general x34, starting transfers between devices, layer(): gate = jnp.dot(a, w['w_gate'], preferred_element_type=jnp.float32)  48.2 us
    dot_general x34, waiting for transfers between devices, layer(): gate = jnp.dot(a, w['w_gate'], preferred_element_type=jnp.float32)  47 us
  transfers between devices with their start and end apart: 105, of which 39 were waited for; matrix products, arithmetic and copies ran while one was open for 39% of the time, Pallas kernels for 0%

commit v1 on v0

v1 whole, which is shorter than its diff:
```python
import jax
import jax.numpy as jnp
from jax import lax
from jax.sharding import PartitionSpec as P

NAMES = ("w_gate", "w_up", "w_down")


def matmul(a, w):
    return jnp.dot(a, w, preferred_element_type=jnp.float32).astype(jnp.bfloat16)


def normed(h):
    wide = h.astype(jnp.float32)
    scale = lax.rsqrt(jnp.mean(wide**2, -1, keepdims=True) + 1e-6)
    return (wide * scale).astype(jnp.bfloat16)


def layer(h, w):
    a = normed(h)
    gate = jnp.dot(a, w["w_gate"], preferred_element_type=jnp.float32)
    up = jnp.dot(a, w["w_up"], preferred_element_type=jnp.float32)
    return h + matmul((jax.nn.silu(gate) * up).astype(jnp.bfloat16), w["w_down"])


def adamw(w, m, v, g):
    m = 0.9 * m + 0.1 * g
    v = 0.95 * v + 0.05 * g * g
    step = m * lax.rsqrt(v + 1e-8) + 0.1 * w
    return (w - 0.02 * step).astype(jnp.bfloat16), m, v


def solution(mesh):
    size = mesh.shape["dp"]

    def body(x, dy, *arrays):
        weights, m, v = (arrays[i : i + 3] for i in (0, 3, 6))
        layers = weights[0].shape[0]
        per_layer = [{name: w[n] for name, w in zip(NAMES, weights)} for n in range(layers)]

        def stack(per_layer):
            h = x[0]
            for w in per_layer:
                h = layer(h, w)
            return h

        _, back = jax.vjp(stack, per_layer)
        grads = back(dy[0])[0]
        me = lax.axis_index("dp")
        new = {}
        for n in reversed(range(layers)):
            for i, name in enumerate(NAMES):
                g = lax.psum_scatter(grads[n][name], "dp", scatter_dimension=0, tiled=True)
                rows = g.shape[0]
                mine = lax.dynamic_slice_in_dim(weights[i][n], me * rows, rows)
                w1, m1, v1 = adamw(mine.astype(jnp.float32), m[i][n], v[i][n], g.astype(jnp.float32))
                new[n, i] = lax.all_gather(w1, "dp", axis=0, tiled=True), m1, v1
        return tuple(jnp.stack([new[n, i][k] for n in range(layers)]) for k in range(3) for i in range(3))

    seq, whole, rows = P(("rep", "dp"), None, None), P(None, None, None), P(None, "dp", None)
    return jax.shard_map(
        body,
        mesh=mesh,
        in_specs=(seq, seq, whole, whole, whole) + (rows,) * 6,
        out_specs=(P("rep", None, None),) * 3 + (P("rep", "dp", None),) * 6,
        check_vma=False,
    )
```

time: 838 us -> 711 us (0.85)
  waiting for transfers between devices: 133 us -> 421 us
  starting transfers between devices: 161 us -> 0.77 us
  other arithmetic: 133 us -> 32.5 us
  matrix products: 267 us -> 209 us
  loops' own time: 47.7 us -> 0 us
  local copies, waits for them, and re-layouts: 70.2 us -> 24.6 us
    reduce_scatter x0 -> x6, waiting for transfers between devices: none -> 215 us  [body(): g = lax.psum_scatter(grads[n][name], 'dp', scatter_dimension=0, tiled=True)]
    all_gather x0 -> x6, waiting for transfers between devices: none -> 204 us  [body(): new[n, i] = (lax.all_gather(w1, 'dp', axis=0, tiled=True), m1, v1)]
    dot_general x102 -> x0, starting transfers between devices: 161 us -> none  [the longest x34 57.7 us: matmul(): jnp.dot(a, w, preferred_element_type=jnp.float32).astype(jnp.bfloat16)]
    dot_general x112 -> x0, other arithmetic: 97.3 us -> none
    dot_general x102 -> x0, waiting for transfers between devices: 87 us -> none  [the longest x34 47 us: layer(): gate = jnp.dot(a, w['w_gate'], preferred_element_type=jnp.float32)]
    another operation x6 -> x0, loops' own time: 47.7 us -> none  [the longest x2 16.4 us: matmul(): jnp.dot(a, w, preferred_element_type=jnp.float32).astype(jnp.bfloat16)]
    reshape x3 -> x0, waiting for transfers between devices: 45.8 us -> none  [step(): t.reshape(-1, *t.shape[2:])]
    unnamed x45 -> x36, local copies, waits for them, and re-layouts: 55.3 us -> 10.8 us
  transfers between devices with their start and end apart: 105 -> 12, of which waited for: 39 -> 10; matrix products, arithmetic and copies ran while one was open for 39% -> 21% of each run, Pallas kernels for 0% -> 0%
where the time goes in v1:
time: 711 us; the launch traced here: 703 us
  waiting for transfers between devices  421 us (59%)
  matrix products  209 us (29%)
  other arithmetic  32.5 us (5%)
  local copies, waits for them, and re-layouts  24.6 us (3%)
  between operations  14.9 us (2%)
    reduce_scatter x6, waiting for transfers between devices, body(): g = lax.psum_scatter(grads[n][name], 'dp', scatter_dimension=0, tiled=True)  215 us
    all_gather x6, waiting for transfers between devices, body(): new[n, i] = (lax.all_gather(w1, 'dp', axis=0, tiled=True), m1, v1)  204 us
    dot_general x5, matrix products, layer(): gate = jnp.dot(a, w['w_gate'], preferred_element_type=jnp.float32)  79.1 us
    dot_general x5, matrix products, layer(): up = jnp.dot(a, w['w_up'], preferred_element_type=jnp.float32)  74.2 us
    dot_general x5, matrix products, matmul(): jnp.dot(a, w, preferred_element_type=jnp.float32).astype(jnp.bfloat16)  56.2 us
    another operation x6, other arithmetic, body(): jnp.stack([new[n, i][k] for n in range(layers)])  22 us
  transfers between devices with their start and end apart: 12, of which 10 were waited for; matrix products, arithmetic and copies ran while one was open for 21% of the time, Pallas kernels for 0%

profile of v1, /device:TPU:21, one launch (start us, length us, event | category | flops | bytes accessed | tf_op | source)
XLA Modules:
  0.0 702.9 jit_solution(15772414050069729366)
XLA Ops:
  7.3 3.0 copy.20
  10.3 0.6 fusion.15
  10.8 12.7 %fusion.45 = f32[2048,2048]{1,0:T(8,128)} fusion(bf16[1,2048,640]{2,1,0:T(8,128)(2,1)} %param.11, f32[2048]{0:T(1024)S(1)} %add_rsqrt_fusion, bf16[2,640,2048]{2,1,0:T(8,128)(2,1)} %param.13), kind=kOutput, calls=%fused_computation.68 | convolution fusion | flops 5372641280 | bytes 22028288 | tf_op jit(solution)/shard_map/jvp()/dot_general | solution.py:21
  23.5 16.8 %multiply_convert_fusion.1 = (bf16[2048,2048]{1,0:T(8,128)(2,1)}, f32[2048,2048]{1,0:T(8,128)}) fusion(f32[2048,2048]{1,0:T(8,128)} %fusion.45, bf16[2,640,2048]{2,1,0:T(8,128)(2,1)} %param.14, bf16[1,2048,640]{2,1,0:T(8,128)(2,1)} %param.11, f32[2048]{0:T(1024)S(1)} %add_rsqrt_fusion), kind=kOutput, calls=%fused_computation.17 | convolution fusion | flops 5397807104 | bytes 47194112 | tf_op jit(solution)/shard_map/jvp()/dot_general | solution.py:22
  40.3 9.3 %fusion.19 = (f32[2048]{0:T(1024)S(1)}, bf16[2048,640]{0,1:T(8,128)(2,1)S(1)}) fusion(bf16[2048,2048]{1,0:T(8,128)(2,1)} %get-tuple-element.33, bf16[2,2048,640]{2,1,0:T(8,128)(2,1)} %param.15, bf16[1,2048,640]{1,2,0:T(8,128)(2,1)S(1)} %copy.20), kind=kOutput, calls=%fused_computation.37 | convolution fusion | flops 5375260672 | bytes 16261120 | tf_op jit(solution)/shard_map/jvp()/dot_general | solution.py:10
  49.6 11.6 %convolution_convert_fusion.1 = bf16[2048,2048]{1,0:T(8,128)(2,1)} fusion(bf16[1,2048,640]{2,1,0:T(8,128)(2,1)S(1)} %copy-done.6, bf16[2,2048,640]{2,1,0:T(8,128)(2,1)} %param.15), kind=kOutput, calls=%fused_computation.29 | convolution fusion | flops 5372903424 | bytes 13631488 | tf_op jit(solution)/shard_map/transpose(jvp())/dot_general | solution.py:10
  61.2 12.0 %fusion.34 = f32[2048,2048]{1,0:T(8,128)} fusion(bf16[2048,640]{0,1:T(8,128)(2,1)S(1)} %get-tuple-element.36, f32[2048]{0:T(1024)S(1)} %fusion.102, bf16[2,640,2048]{2,1,0:T(8,128)(2,1)} %param.14), kind=kOutput, calls=%fused_computation.57 | convolution fusion | flops 5372641280 | bytes 22028288 | tf_op jit(solution)/shard_map/jvp()/dot_general | solution.py:22
  73.2 25.1 %fusion.2 = (bf16[2048,2048]{1,0:T(8,128)(2,1)}, f32[2048,2048]{1,0:T(8,128)}) fusion(f32[2048,2048]{1,0:T(8,128)} %fusion.34, bf16[2048,2048]{1,0:T(8,128)(2,1)} %convolution_convert_fusion.1, bf16[2,640,2048]{2,1,0:T(8,128)(2,1)} %param.13, bf16[2048,640]{0,1:T(8,128)(2,1)} %copy-done.2, f32[2048]{0:T(1024)S(1)} %fusion.102), kind=kOutput, calls=%fused_computation.8 | convolution fusion | flops 5422972928 | bytes 55582720 | tf_op jit(solution)/shard_map/jvp()/dot_general | solution.py:21
  98.3 15.5 %fusion.22 = bf16[2048,640]{1,0:T(8,128)(2,1)} fusion(f32[2048,2048]{1,0:T(8,128)} %fusion.34, bf16[1,2048,640]{2,1,0:T(8,128)(2,1)S(1)} %copy-done.7, f32[2048,2048]{1,0:T(8,128)} %get-tuple-element.38), kind=kOutput, calls=%fused_computation.44 | convolution fusion | flops 5395185664 | bytes 38797312 | tf_op jit(solution)/shard_map/transpose(jvp())/dot_general | solution.py:10
  114.0 21.8 %fusion.23 = bf16[2048,640]{0,1:T(8,128)(2,1)} fusion(bf16[2048,2048]{1,0:T(8,128)(2,1)} %convolution_convert_fusion.1, bf16[2,640,2048]{2,1,0:T(8,128)(2,1)} %param.14, f32[2048,2048]{1,0:T(8,128)} %get-tuple-element.38), kind=kOutput, calls=%fused_computation.45 | convolution fusion | flops 5395185664 | bytes 30408704 | tf_op jit(solution)/shard_map/transpose(jvp())/dot_general | solution.py:22
  135.8 3.0 copy.21
  138.8 11.4 %fusion.21 = (f32[2048]{0:T(1024)S(1)}, bf16[2048,640]{0,1:T(8,128)(2,1)S(1)}) fusion(bf16[2048,640]{0,1:T(8,128)(2,1)} %copy-done.2, bf16[2048,640]{0,1:T(8,128)(2,1)} %fusion.23, bf16[2048,2048]{1,0:T(8,128)(2,1)} %get-tuple-element.37, bf16[2,640,2048]{2,1,0:T(8,128)(2,1)} %param.13), kind=kOutput, calls=%fused_computation.39 | convolution fusion | flops 5375260672 | bytes 18882560 | tf_op jit(solution)/shard_map/transpose(jvp())/dot_general | solution.py:21
  150.2 1.8 fusion.31
  152.1 1.5 copy-done.5
  153.6 10.5 %convolution_convert_fusion.2 = bf16[2048,640]{1,0:T(8,128)(2,1)} fusion(bf16[2048,2048]{1,0:T(8,128)(2,1)} %get-tuple-element.33, bf16[2048,640]{0,1:T(8,128)(2,1)S(1)} %fusion.31), kind=kOutput, calls=%fused_computation.49 | convolution fusion | flops 5370019840 | bytes 13631488 | tf_op jit(solution)/shard_map/transpose(jvp())/dot_general | solution.py:10
  164.2 12.7 %fusion.24 = bf16[640,2048]{1,0:T(8,128)(2,1)} fusion(bf16[2048,2048]{1,0:T(8,128)(2,1)} %convolution_convert_fusion.1, bf16[2048,640]{0,1:T(8,128)(2,1)S(1)} %copy-done.4, f32[2048]{0:T(1024)S(1)} %fusion.102, f32[2048,2048]{1,0:T(8,128)} %get-tuple-element.38), kind=kOutput, calls=%fused_computation.46 | convolution fusion | flops 5399117824 | bytes 30416896 | tf_op jit(solution)/shard_map/transpose(jvp())/dot_general | solution.py:22
  177.1 9.3 %convolution_convert_fusion = bf16[2048,2048]{1,0:T(8,128)(2,1)S(1)} fusion(bf16[2048,640]{0,1:T(8,128)(2,1)} %copy-done.5, bf16[2,2048,640]{2,1,0:T(8,128)(2,1)} %param.15), kind=kOutput, calls=%fused_computation.28 | convolution fusion | flops 5372903424 | bytes 13631488 | tf_op jit(solution)/shard_map/transpose(jvp())/dot_general | solution.py:10
  186.4 3.2 copy-done.16
  189.7 10.9 %fusion.28 = bf16[640,2048]{1,0:T(8,128)(2,1)} fusion(bf16[2048,2048]{1,0:T(8,128)(2,1)S(1)} %convolution_convert_fusion, f32[2048,2048]{1,0:T(8,128)} %fusion.45, bf16[1,2048,640]{1,2,0:T(8,128)(2,1)S(1)} %copy-done.1, f32[2048]{0:T(1024)S(1)} %copy-done.15), kind=kOutput, calls=%fused_computation.48 | convolution fusion | flops 5399117824 | bytes 30416896 | tf_op jit(solution)/shard_map/transpose(jvp())/dot_general | solution.py:22
  200.7 10.9 %convolution_convert_fusion.3 = bf16[640,2048]{1,0:T(8,128)(2,1)} fusion(bf16[2048,2048]{1,0:T(8,128)(2,1)} %get-tuple-element.37, bf16[2048,640]{0,1:T(8,128)(2,1)} %copy-done.2, f32[2048]{0:T(1024)S(1)} %fusion.102), kind=kOutput, calls=%fused_computation.50 | convolution fusion | flops 5372641280 | bytes 13639680 | tf_op jit(solution)/shard_map/transpose(jvp())/dot_general | solution.py:21
  211.6 0.1 reduce-scatter.7.cloned.1.call-start
  211.7 19.1 %fusion.25 = bf16[640,2048]{1,0:T(8,128)(2,1)} fusion(f32[2048,2048]{1,0:T(8,128)} %fusion.45, f32[2048,2048]{1,0:T(8,128)} %get-tuple-element.34, bf16[2048,2048]{1,0:T(8,128)(2,1)} %copy-done.16, bf16[1,2048,640]{1,2,0:T(8,128)(2,1)S(1)} %copy-done.1, f32[2048]{0:T(1024)S(1)} %copy-done.15), kind=kOutput, calls=%fused_computation.47 | convolution fusion | flops 5420089344 | bytes 47194112 | tf_op jit(solution)/shard_map/transpose(jvp())/dot_general | solution.py:21
  230.8 0.1 all-gather.15.cloned.1.call-start
  230.9 4.5 fusion.117
  235.3 2.6 fusion.80
  238.1 0.7 all-gather.17.cloned.1.call-update
  238.9 4.7 fusion.118
  243.6 46.4 %reduce-scatter.13.cloned.1.call-done = bf16[40,2048]{1,0:T(8,128)(2,1)} async-done(((bf16[640,2048]{1,0:T(8,128)(2,1)}), bf16[40,2048]{1,0:T(8,128)(2,1)}) %reduce-scatter.13.cloned.1.call-update) | async-done | bytes 163856 | tf_op jit(solution)/shard_map/reduce_scatter | solution.py:53
  290.1 58.8 %reduce-scatter.11.cloned.1.call-done = bf16[40,2048]{1,0:T(8,128)(2,1)} async-done(((bf16[640,2048]{1,0:T(8,128)(2,1)}), bf16[40,2048]{1,0:T(8,128)(2,1)}) %reduce-scatter.11.cloned.1.call-update) | async-done | bytes 163856 | tf_op jit(solution)/shard_map/reduce_scatter | solution.py:53
  348.9 2.8 fusion.74
  351.9 0.6 all-gather.13.cloned.1.call-update
  352.5 4.7 fusion.119
  357.2 50.6 %reduce-scatter.9.cloned.1.call-done = bf16[40,2048]{1,0:T(8,128)(2,1)} async-done(((bf16[640,2048]{1,0:T(8,128)(2,1)}), bf16[40,2048]{1,0:T(8,128)(2,1)}) %reduce-scatter.9.cloned.1.call-update) | async-done | bytes 163856 | tf_op jit(solution)/shard_map/reduce_scatter | solution.py:53
  407.8 58.8 %reduce-scatter.7.cloned.1.call-done = bf16[40,2048]{1,0:T(8,128)(2,1)} async-done(((bf16[640,2048]{1,0:T(8,128)(2,1)}), bf16[40,2048]{1,0:T(8,128)(2,1)}) %reduce-scatter.7.cloned.1.call-update) | async-done | bytes 163856 | tf_op jit(solution)/shard_map/reduce_scatter | solution.py:53
  466.6 2.7 fusion.68
  469.5 0.6 all-gather.9.cloned.1.call-update
  470.1 2.2 pad_maximum_fusion.5
  472.3 2.4 pad_maximum_fusion.4
  474.8 1.1 pad_maximum_fusion.3
  475.9 30.9 %all-gather.15.cloned.1.call-done = bf16[2048,640]{1,0:T(8,128)(2,1)} async-done(((bf16[128,640]{1,0:T(8,128)(2,1)}), bf16[2048,640]{1,0:T(8,128)(2,1)}) %all-gather.15.cloned.1.call-update) | async-done | bytes 2621456 | tf_op jit(solution)/shard_map/all_gather | solution.py:57
  506.8 36.7 %all-gather.17.cloned.1.call-done = bf16[2048,640]{1,0:T(8,128)(2,1)} async-done(((bf16[128,640]{1,0:T(8,128)(2,1)}), bf16[2048,640]{1,0:T(8,128)(2,1)}) %all-gather.17.cloned.1.call-update) | async-done | bytes 2621456 | tf_op jit(solution)/shard_map/all_gather | solution.py:57
  543.5 5.4 pad_maximum_fusion.2
  549.0 31.3 %all-gather.11.cloned.1.call-done = bf16[640,2048]{1,0:T(8,128)(2,1)} async-done(((bf16[40,2048]{1,0:T(8,128)(2,1)}), bf16[640,2048]{1,0:T(8,128)(2,1)}) %all-gather.11.cloned.1.call-update) | async-done | bytes 2621456 | tf_op jit(solution)/shard_map/all_gather | solution.py:57
  580.3 36.6 %all-gather.13.cloned.1.call-done = bf16[640,2048]{1,0:T(8,128)(2,1)} async-done(((bf16[40,2048]{1,0:T(8,128)(2,1)}), bf16[640,2048]{1,0:T(8,128)(2,1)}) %all-gather.13.cloned.1.call-update) | async-done | bytes 2621456 | tf_op jit(solution)/shard_map/all_gather | solution.py:57
  616.9 5.4 pad_maximum_fusion.1
  622.3 31.4 %all-gather.7.cloned.1.call-done = bf16[640,2048]{1,0:T(8,128)(2,1)} async-done(((bf16[40,2048]{1,0:T(8,128)(2,1)}), bf16[640,2048]{1,0:T(8,128)(2,1)}) %all-gather.7.cloned.1.call-update) | async-done | bytes 2621456 | tf_op jit(solution)/shard_map/all_gather | solution.py:57
  653.6 36.6 %all-gather.9.cloned.1.call-done = bf16[640,2048]{1,0:T(8,128)(2,1)} async-done(((bf16[40,2048]{1,0:T(8,128)(2,1)}), bf16[640,2048]{1,0:T(8,128)(2,1)}) %all-gather.9.cloned.1.call-update) | async-done | bytes 2621456 | tf_op jit(solution)/shard_map/all_gather | solution.py:57
  690.3 5.4 pad_maximum_fusion
  (56 shorter events, 1.2 us)
Async XLA Ops:
  7.2 228.2 %reduce-scatter.17.cloned.1.call-start = ((), (), s32[]{:S(2)}) async-start(), calls=%async_computation.16 | async-start | bytes 2785280 | tf_op jit(solution)/shard_map/reduce_scatter | solution.py:53
  10.3 30.0 %copy-start = (bf16[1,2048,640]{1,2,0:T(8,128)(2,1)}, bf16[1,2048,640]{1,2,0:T(8,128)(2,1)S(1)}, u32[]{:S(2)}) copy-start(bf16[1,2048,640]{1,2,0:T(8,128)(2,1)S(1)} %copy.20) | copy-start | bytes 7864324
  10.8 12.7 %copy-start.14 = (f32[2048]{0:T(1024)}, f32[2048]{0:T(1024)S(1)}, u32[]{:S(2)}) copy-start(f32[2048]{0:T(1024)S(1)} %add_rsqrt_fusion) | copy-start | bytes 24580
  40.3 9.3 %copy-start.6 = (bf16[1,2048,640]{2,1,0:T(8,128)(2,1)S(1)}, bf16[1,2048,640]{2,1,0:T(8,128)(2,1)}, u32[]{:S(2)}) copy-start(bf16[1,2048,640]{2,1,0:T(8,128)(2,1)} %param.12) | copy-start | bytes 7864324
  49.6 11.6 %copy-start.12 = (f32[2048]{0:T(1024)}, f32[2048]{0:T(1024)S(1)}, u32[]{:S(2)}) copy-start(f32[2048]{0:T(1024)S(1)} %get-tuple-element.35) | copy-start | bytes 24580
  49.6 11.6 %copy-start.2 = (bf16[2048,640]{0,1:T(8,128)(2,1)}, bf16[2048,640]{0,1:T(8,128)(2,1)S(1)}, u32[]{:S(2)}) copy-start(bf16[2048,640]{0,1:T(8,128)(2,1)S(1)} %get-tuple-element.36) | copy-start | bytes 7864324
  73.2 25.1 %copy-start.7 = (bf16[1,2048,640]{2,1,0:T(8,128)(2,1)S(1)}, bf16[1,2048,640]{2,1,0:T(8,128)(2,1)}, u32[]{:S(2)}) copy-start(bf16[1,2048,640]{2,1,0:T(8,128)(2,1)} %param.12) | copy-start | bytes 7864324
  113.9 121.4 %reduce-scatter.15.cloned.1.call-start = ((), (), s32[]{:S(2)}) async-start(), calls=%async_computation.14 | async-start | bytes 2785280 | tf_op jit(solution)/shard_map/reduce_scatter | solution.py:53
  138.8 11.4 %copy-start.13 = (f32[2048]{0:T(1024)S(1)}, f32[2048]{0:T(1024)}, u32[]{:S(2)}) copy-start(f32[2048]{0:T(1024)} %copy-done.12) | copy-start | bytes 24580
  138.8 11.4 %copy-start.3 = (bf16[2048,640]{0,1:T(8,128)(2,1)S(1)}, bf16[2048,640]{0,1:T(8,128)(2,1)}, u32[]{:S(2)}) copy-start(bf16[2048,640]{0,1:T(8,128)(2,1)} %copy-done.2) | copy-start | bytes 7864324
  152.1 1.5 copy-start.5
  153.6 10.6 %copy-start.4 = (bf16[2048,640]{0,1:T(8,128)(2,1)S(1)}, bf16[2048,640]{0,1:T(8,128)(2,1)}, u32[]{:S(2)}) copy-start(bf16[2048,640]{0,1:T(8,128)(2,1)} %copy-done.2) | copy-start | bytes 7864324
  164.1 126.0 %reduce-scatter.13.cloned.1.call-start = ((), (), s32[]{:S(2)}) async-start(), calls=%async_computation.12 | async-start | bytes 2785280 | tf_op jit(solution)/shard_map/reduce_scatter | solution.py:53
  177.0 12.7 %copy-start.1 = (bf16[1,2048,640]{1,2,0:T(8,128)(2,1)S(1)}, bf16[1,2048,640]{1,2,0:T(8,128)(2,1)}, u32[]{:S(2)}) copy-start(bf16[1,2048,640]{1,2,0:T(8,128)(2,1)} %copy-done) | copy-start | bytes 7864324
  177.0 12.7 %copy-start.15 = (f32[2048]{0:T(1024)S(1)}, f32[2048]{0:T(1024)}, u32[]{:S(2)}) copy-start(f32[2048]{0:T(1024)} %copy-done.14) | copy-start | bytes 24580
  177.0 171.9 %reduce-scatter.11.cloned.1.call-start = ((), (), s32[]{:S(2)}) async-start(), calls=%async_computation.10 | async-start | bytes 2785280 | tf_op jit(solution)/shard_map/reduce_scatter | solution.py:53
  186.4 3.3 copy-start.16
  200.6 207.1 %reduce-scatter.9.cloned.1.call-start = ((), (), s32[]{:S(2)}) async-start(), calls=%async_computation.8 | async-start | bytes 2785280 | tf_op jit(solution)/shard_map/reduce_scatter | solution.py:53
  211.6 255.0 %reduce-scatter.7.cloned.1.call-start = ((), (), s32[]{:S(2)}) async-start(), calls=%async_computation.6 | async-start | bytes 2785280 | tf_op jit(solution)/shard_map/reduce_scatter | solution.py:53
  230.8 276.0 %all-gather.15.cloned.1.call-start = ((), (), s32[]{:S(2)}) async-start(), calls=%async_computation.15 | async-start | bytes 2785280 | tf_op jit(solution)/shard_map/all_gather | solution.py:57
  238.1 305.5 %all-gather.17.cloned.1.call-start = ((), (), s32[]{:S(2)}) async-start(), calls=%async_computation.17 | async-start | bytes 2785280 | tf_op jit(solution)/shard_map/all_gather | solution.py:57
  238.9 341.4 %all-gather.11.cloned.1.call-start = ((), (), s32[]{:S(2)}) async-start(), calls=%async_computation.11 | async-start | bytes 2785280 | tf_op jit(solution)/shard_map/all_gather | solution.py:57
  351.8 265.1 %all-gather.13.cloned.1.call-start = ((), (), s32[]{:S(2)}) async-start(), calls=%async_computation.13 | async-start | bytes 2785280 | tf_op jit(solution)/shard_map/all_gather | solution.py:57
  352.4 301.2 %all-gather.7.cloned.1.call-start = ((), (), s32[]{:S(2)}) async-start(), calls=%async_computation.7 | async-start | bytes 2785280 | tf_op jit(solution)/shard_map/all_gather | solution.py:57
  469.3 5.4 copy-start.8
  469.3 5.4 copy-start.9
  469.4 5.4 copy-start.10
  469.4 5.4 copy-start.11
  469.4 220.8 %all-gather.9.cloned.1.call-start = ((), (), s32[]{:S(2)}) async-start(), calls=%async_computation.9 | async-start | bytes 2785280 | tf_op jit(solution)/shard_map/all_gather | solution.py:57
Sparse Core Ops, SparseCore 0:
  114.1 59.1 reduce-scatter.16
  175.6 56.0 reduce-scatter.14
  234.0 56.0 reduce-scatter.12
  292.8 56.0 reduce-scatter.10
  351.7 56.0 reduce-scatter.8
  410.5 56.0 reduce-scatter.6
  468.2 38.5 all-gather.14
  508.4 35.0 all-gather.16
  545.2 35.0 all-gather.10
  581.8 35.0 all-gather.12
  618.5 35.0 all-gather.6
  655.1 35.0 all-gather.8

commit v2 on v1

v2 whole, which is shorter than its diff:
```python
import functools

import jax
import jax.numpy as jnp
from jax import lax
from jax.experimental import pallas as pl
from jax.experimental.pallas import tpu as pltpu
from jax.sharding import PartitionSpec as P

MESH = pl.DeviceIdType.MESH
BF, F32 = jnp.bfloat16, jnp.float32
BLOCK = 256
STRIPS = 4
POINTS = 3
ANY = pl.BlockSpec(memory_space=pl.ANY)


def dot(a, b, dims=((1,), (0,))):
    return lax.dot_general(a, b, (dims, ((), ())), preferred_element_type=F32)


def scale_of(wide):
    return lax.rsqrt(jnp.mean(wide * wide, -1, keepdims=True) + 1e-6)


def forward(x_ref, dy_ref, wg_ref, wu_ref, wd_ref, a_ref, at_ref, h_ref, b_ref, bt_ref, dyt_ref, act_ref):
    wide = x_ref[...].astype(F32)
    a = wide * scale_of(wide)
    at_ref[...] = a.T.astype(BF)
    a = a.astype(BF)
    a_ref[...] = a
    width = wg_ref.shape[1] // STRIPS
    for j in range(STRIPS):
        cols = slice(j * width, (j + 1) * width)
        gate, up = dot(a, wg_ref[:, cols]), dot(a, wu_ref[:, cols])
        act_ref[:, cols] = (gate * jax.nn.sigmoid(gate) * up).astype(BF)
    down = dot(act_ref[...], wd_ref[...]).astype(BF)
    h = (wide + down.astype(F32)).astype(BF)
    h_ref[...] = h
    wide = h.astype(F32)
    b = wide * scale_of(wide)
    bt_ref[...] = b.T.astype(BF)
    b_ref[...] = b.astype(BF)
    dyt_ref[...] = dy_ref[...].astype(F32).T.astype(BF)


def adamw(w, m, v, g):
    m = 0.9 * m + 0.1 * g
    v = 0.95 * v + 0.05 * g * g
    step = m * lax.rsqrt(v + 1e-8) + 0.1 * w
    return (w - 0.02 * step).astype(BF), m, v


def backward(
    n, b_ref, bt_ref, dyi_ref, dyti_ref, h_ref, a_ref, at_ref, wg_ref, wu_ref, wd_ref,
    mg_ref, mu_ref, md_ref, vg_ref, vu_ref, vd_ref,
    ng_ref, nu_ref, nd_ref, omg_ref, omu_ref, omd_ref, ovg_ref, ovu_ref, ovd_ref,
    act, actt, dy, dyt, wg, wu, wd, dgu, prod, own_g, got_g, own_d, got_d, slot_g, slot_d,
    wo_g, wo_d, m_g, v_g, m_d, v_d,
    load, opt_load, pair_send, pair_got, rs_send, rs_got, ag_send, ag_got, fw_send, fw_got, keep_w, keep_m, keep_v,
    dpair_send, dpair_got, drs_send, drs_got, dag_send, dag_got, dfw_send, dfw_got, dkeep_w, dkeep_m, dkeep_v, credit,
):
    chips = n // 2
    tokens, d = dy.shape
    ff = wg.shape[1]
    width = ff // STRIPS
    rows, drows = d // n, ff // n
    half = drows // 2
    layers = wg_ref.shape[0]
    blocks = tokens // BLOCK
    turns = STRIPS + 1
    last = layers * turns - 2

    me = lax.axis_index("dp")
    z, c = me // 2, me % 2
    near = (((z + 1) % chips) * 2 + c, ((z + chips - 1) % chips) * 2 + c)
    mate = z * 2 + (1 - c)

    barrier = pltpu.get_barrier_semaphore()
    for other in (*near, mate):
        pl.semaphore_signal(barrier, inc=1, device_id={"dp": other}, device_id_type=MESH)
    pl.semaphore_wait(barrier, 3)

    def fetch(src, dst, k):
        return pltpu.make_async_copy(src, dst, load.at[k])

    top = layers - 1

    def loads(layer, acts, actst):
        return (
            fetch(acts, act, 0), fetch(wg_ref.at[layer], wg, 1), fetch(wu_ref.at[layer], wu, 2),
            fetch(wd_ref.at[layer], wd, 3), fetch(actst, actt, 4),
        )

    first = (*loads(top, b_ref, bt_ref), fetch(dyi_ref, dy, 5), fetch(dyti_ref, dyt, 6))
    for k in (0, 1, 2, 5, 3, 4, 6):
        first[k].start()
    mine = pl.ds(pl.multiple_of(me * rows, 8), rows)
    dmine = pl.ds(pl.multiple_of(me * drows, 8), drows)
    params = [
        (wg_ref.at[:, mine], wo_g.at[0]), (wu_ref.at[:, mine], wo_g.at[1]), (wd_ref.at[:, dmine], wo_d),
        (mg_ref, m_g.at[0]), (mu_ref, m_g.at[1]), (md_ref, m_d),
        (vg_ref, v_g.at[0]), (vu_ref, v_g.at[1]), (vd_ref, v_d),
    ]
    params = [pltpu.make_async_copy(s, t, opt_load.at[k]) for k, (s, t) in enumerate(params)]
    for copy in params:
        copy.start()

    second = loads(0, a_ref, at_ref)
    states = fetch(h_ref, act, 0)

    def remote(src, dst, send, got, to):
        return pltpu.make_async_remote_copy(src, dst, send, got, device_id={"dp": to}, device_id_type=MESH)

    def tok(t):
        return pl.ds(pl.multiple_of(t * BLOCK, BLOCK), BLOCK)

    def strip_block(j, t):
        cols = pl.ds(pl.multiple_of(j * width, width), width)
        a = act[tok(t), :]
        gate = dot(a, wg[:, cols])
        up = dot(a, wu[:, cols])
        dact = dot(dy[tok(t), :], wd[cols, :], ((1,), (1,))).astype(BF).astype(F32)
        sig = jax.nn.sigmoid(gate)
        silu = gate * sig
        prod[tok(t), :] = (silu * up).astype(BF)
        dgu[0, tok(t), cols] = (dact * up * (sig + silu * (1.0 - sig))).astype(BF)
        dgu[1, tok(t), cols] = (dact * silu).astype(BF)

    pieces = width // 256

    def weight_rows(j, k, piece):
        cols = pl.ds(pl.multiple_of(j * width + piece * 256, 256), 256)
        out = pl.ds(pl.multiple_of(piece * 256, 256), 256)
        total = dot(actt[...], dgu[k, :, cols])
        for chip in range(chips):
            for core in range(2):
                at = (chip * 2 + core) * rows
                own_g[j, core, k, chip, :, out] = total[at : at + rows].astype(BF)

    def down_rows(r, j, piece):
        total = dot(dyt[...], prod[:, pl.ds(pl.multiple_of(piece * 256, 256), 256)])
        total = total.T.astype(BF)
        per = 256 // (2 * drows)
        for k in range(per):
            for core in range(2):
                at = (k * 2 + core) * drows
                own_d[r, core, (j * pieces + piece) * per + k] = total[at : at + drows]

    def state_block(t):
        by_gate = dot(dgu[0, tok(t), :], wg[...], ((1,), (1,))).astype(BF)
        by_up = dot(dgu[1, tok(t), :], wu[...], ((1,), (1,))).astype(BF)
        by_a = (by_gate.astype(F32) + by_up.astype(F32)).astype(BF).astype(F32)
        wide = act[tok(t), :].astype(F32)
        scale = scale_of(wide)
        lean = jnp.mean(by_a * wide, -1, keepdims=True)
        by_h = (by_a * scale - wide * (scale * scale * scale * lean)).astype(BF)
        total = dy[tok(t), :].astype(F32) + by_h.astype(F32)
        dy[tok(t), :] = total.astype(BF)
        dyt[:, tok(t)] = total.astype(BF).astype(F32).T.astype(BF)

    def strip_outs(layer, j):
        return pl.ds(pl.multiple_of(j * width, width), width), (ng_ref, nu_ref)

    def block_of(k, chip):
        return pl.ds(pl.multiple_of((chip * 2 + c) * rows, 8), rows)

    def dblock_of(k, chip):
        return pl.ds(pl.multiple_of((chip * 2 + c) * drows + k * half, 8), half)

    def wrap(v):
        return lax.rem(v + 2 * chips, chips)

    def hop(k, step):
        return wrap(z - 1 - step) if k == 0 else wrap(z + 1 + step)

    def ag_hop(k, step):
        return wrap(z - step) if k == 0 else wrap(z + step)

    def ring_step(o, layer, j, q):
        for k in range(2):
            b = hop(k, o)
            mate_part = got_g[j, k, b].astype(F32) + own_g[j, c, k, b].astype(F32)

            @pl.when(o == 0)
            def _():
                slot_g[q, k, chips - 1] = mate_part.astype(BF)
                remote(slot_g.at[q, k, chips - 1], slot_g.at[q, k, 0], rs_send.at[q, k], rs_got.at[q, k, 0], near[k]).start()

            @pl.when(o > 0)
            def _():
                here = slot_g.at[q, k, o - 1]
                pltpu.make_async_copy(here, here, rs_got.at[q, k, o - 1]).wait()
                here[...] = (here[...].astype(F32) + mate_part).astype(BF)
                remote(here, slot_g.at[q, k, o], rs_send.at[q, k], rs_got.at[q, k, o], near[k]).start()

    def dring_step(o, layer, r):
        for k in range(2):
            b = hop(k, o)
            part = pl.ds(k * half, half)
            mate_part = got_d[b, part].astype(F32) + own_d[r, c, b, part].astype(F32)

            @pl.when(o == 0)
            def _():
                slot_d[r, k, chips - 1] = mate_part.astype(BF)
                remote(slot_d.at[r, k, chips - 1], slot_d.at[r, k, 0], drs_send.at[r, k], drs_got.at[r, k, 0], near[k]).start()

            @pl.when(o > 0)
            def _():
                here = slot_d.at[r, k, o - 1]
                pltpu.make_async_copy(here, here, drs_got.at[r, k, o - 1]).wait()
                here[...] = (here[...].astype(F32) + mate_part).astype(BF)
                remote(here, slot_d.at[r, k, o], drs_send.at[r, k], drs_got.at[r, k, o], near[k]).start()

    def publish(src, dst, keep, send, got, fsend, fgot, to):
        pltpu.make_async_copy(src, dst, keep).start()
        remote(src, dst, send, got, to).start()
        remote(src, dst, fsend, fgot, mate).start()

    def own_step(layer, j, q):
        cols, outs = strip_outs(layer, j)
        for k in range(2):
            here = slot_g.at[q, k, chips - 2]
            pltpu.make_async_copy(here, here, rs_got.at[q, k, chips - 2]).wait()
            mate_part = got_g[j, k, z].astype(F32) + own_g[j, c, k, z].astype(F32)
            g = (here[...].astype(F32) + mate_part).astype(BF).astype(F32)
            w1, m1, v1 = adamw(wo_g[k, layer, :, cols].astype(F32), m_g[k, layer, :, cols], v_g[k, layer, :, cols], g)
            m_g[k, layer, :, cols], v_g[k, layer, :, cols], here[...] = m1, v1, w1
            pltpu.make_async_copy(m_g.at[k, layer, :, cols], (omg_ref, omu_ref)[k].at[layer, :, cols], keep_m.at[q, k]).start()
            pltpu.make_async_copy(v_g.at[k, layer, :, cols], (ovg_ref, ovu_ref)[k].at[layer, :, cols], keep_v.at[q, k]).start()
            publish(
                here, outs[k].at[layer, block_of(k, z), cols], keep_w.at[q, k],
                ag_send.at[q, k], ag_got.at[q, k, 0], fw_send.at[q, k], fw_got.at[q, k], near[k],
            )

    def down_own_step(layer, r):
        for k in range(2):
            part = pl.ds(k * half, half)
            here = slot_d.at[r, k, chips - 2]
            pltpu.make_async_copy(here, here, drs_got.at[r, k, chips - 2]).wait()
            mate_part = got_d[z, part].astype(F32) + own_d[r, c, z, part].astype(F32)
            g = (here[...].astype(F32) + mate_part).astype(BF).astype(F32)
            w1, m1, v1 = adamw(wo_d[layer, part].astype(F32), m_d[layer, part], v_d[layer, part], g)
            m_d[layer, part], v_d[layer, part], here[...] = m1, v1, w1
            pltpu.make_async_copy(m_d.at[layer, part], omd_ref.at[layer, part], dkeep_m.at[r, k]).start()
            pltpu.make_async_copy(v_d.at[layer, part], ovd_ref.at[layer, part], dkeep_v.at[r, k]).start()
            publish(
                here, nd_ref.at[layer, dblock_of(k, z)], dkeep_w.at[r, k],
                dag_send.at[r, k], dag_got.at[r, k, 0], dfw_send.at[r, k], dfw_got.at[r, k], near[k],
            )

    def gather_step(s, layer, j, q):
        cols, outs = strip_outs(layer, j)
        for k in range(2):
            here = outs[k].at[layer, block_of(k, ag_hop(k, s)), cols]
            pltpu.make_async_copy(here, here, ag_got.at[q, k, s - 1]).wait()

            @pl.when(s < chips - 1)
            def _():
                remote(here, here, ag_send.at[q, k], ag_got.at[q, k, s], near[k]).start()

            remote(here, here, fw_send.at[q, k], fw_got.at[q, k], mate).start()

    def down_gather_step(s, layer, r):
        for k in range(2):
            here = nd_ref.at[layer, dblock_of(k, ag_hop(k, s))]
            pltpu.make_async_copy(here, here, dag_got.at[r, k, s - 1]).wait()

            @pl.when(s < chips - 1)
            def _():
                remote(here, here, dag_send.at[r, k], dag_got.at[r, k, s], near[k]).start()

            remote(here, here, dfw_send.at[r, k], dfw_got.at[r, k], mate).start()

    steps = 2 * chips - 1
    lags = steps // POINTS

    def point(i, p):
        def lag_step(idx, carry):
            lag = lags - idx
            g = i - lag
            r, j = g // turns, g % turns
            o = (lag - 1) * POINTS + p
            layer, q = top - r, r * STRIPS + j

            @pl.when((g >= 0) & (g <= last) & (j < STRIPS))
            def _():
                @pl.when(o == 0)
                def _():
                    pltpu.make_async_copy(got_g.at[j], got_g.at[j], pair_got.at[q]).wait()

                @pl.when(o < chips - 1)
                def _():
                    ring_step(o, layer, j, q)

                @pl.when(o == chips - 1)
                def _():
                    @pl.when(g == 0)
                    def _():
                        for copy in params:
                            copy.wait()

                    own_step(layer, j, q)

                @pl.when(o > chips - 1)
                def _():
                    gather_step(o - (chips - 1), layer, j, q)

                @pl.when(j == STRIPS - 1)
                def _():
                    @pl.when(o == 0)
                    def _():
                        pltpu.make_async_copy(got_d, got_d, dpair_got.at[r]).wait()

                    @pl.when(o < chips - 1)
                    def _():
                        dring_step(o, layer, r)

                    @pl.when(o == chips - 1)
                    def _():
                        down_own_step(layer, r)

                    @pl.when(o > chips - 1)
                    def _():
                        down_gather_step(o - (chips - 1), layer, r)

                @pl.when((o == chips - 1) & (r < layers - 1))
                def _():
                    pl.semaphore_signal(credit, inc=1, device_id={"dp": mate}, device_id_type=MESH)

            return carry

        lax.fori_loop(0, lags, lag_step, 0)

    def pair_copy(j, q):
        return remote(own_g.at[j, 1 - c], got_g.at[j], pair_send.at[q], pair_got.at[q], mate)

    def dpair_copy(r):
        return remote(own_d.at[r, 1 - c], got_d, dpair_send.at[r], dpair_got.at[r], mate)

    cut = (0, blocks // 2, blocks)

    def segment(i, p):
        r, j = i // turns, i % turns
        q = r * STRIPS + j
        strip = (i <= last) & (j < STRIPS)

        @pl.when((i == 0) & (p == 0))
        def _():
            for k in (0, 1, 2, 3, 5):
                first[k].wait()

        @pl.when((i == turns) & (p == 0))
        def _():
            for k in range(4):
                second[k].wait()

        @pl.when(strip & (p < 2))
        def _():
            def one(t, carry):
                strip_block(j, t)
                return carry

            lax.fori_loop(p * (blocks // 2), (p + 1) * (blocks // 2), one, 0)

        @pl.when(strip & (p == 1))
        def _():
            @pl.when(i == STRIPS - 1)
            def _():
                states.start()

        @pl.when((i == 0) & (p == 1))
        def _():
            for k in (4, 6):
                first[k].wait()

        @pl.when((i == turns) & (p == 1))
        def _():
            second[4].wait()

        @pl.when(strip & (p == 1) & (r > 0))
        def _():
            pair_copy(j, q - STRIPS).wait_send()

            @pl.when(j == 0)
            def _():
                dpair_copy(r - 1).wait_send()

        @pl.when(strip & (p > 0))
        def _():
            def one(e, carry):
                weight_rows(j, e // pieces, e % pieces)
                return carry

            lax.fori_loop((p - 1) * pieces, p * pieces, one, 0)

        @pl.when(strip & (p == POINTS - 1))
        def _():
            def one(e, carry):
                down_rows(r, j, e)
                return carry

            lax.fori_loop(0, pieces, one, 0)

            @pl.when(r > 0)
            def _():
                pl.semaphore_wait(credit, 1)

            pair_copy(j, q).start()

            @pl.when(j == STRIPS - 1)
            def _():
                dpair_copy(r).start()

        @pl.when((i < last) & (j == STRIPS))
        def _():
            @pl.when(p == 0)
            def _():
                second[3].start()
                states.wait()

            def one(t, carry):
                state_block(t)
                return carry

            lax.fori_loop((p * blocks) // POINTS, ((p + 1) * blocks) // POINTS, one, 0)

            @pl.when(p == POINTS - 1)
            def _():
                for k in (0, 1, 2, 4):
                    second[k].start()

    def turn(i, carry):
        def part(p, carry):
            segment(i, p)
            point(i, p)
            return carry

        return lax.fori_loop(0, POINTS, part, carry)

    lax.fori_loop(0, last + 1 + lags, turn, 0)

    def all_of(ref, sem):
        pltpu.make_async_copy(ref, ref, sem).wait()

    def finish(q, carry):
        j = lax.rem(q, STRIPS)
        layer = top - q // STRIPS
        cols, outs = strip_outs(layer, j)

        @pl.when(q >= (layers - 1) * STRIPS)
        def _():
            pair_copy(j, q).wait_send()

        for k in range(2):
            all_of(slot_g.at[q, k, pl.ds(0, chips - 1)], rs_send.at[q, k])
            all_of(slot_g.at[q, k, pl.ds(0, chips - 1)], ag_send.at[q, k])
            all_of(slot_g.at[q, k], fw_send.at[q, k])
            all_of(slot_g.at[q, k], fw_got.at[q, k])
            all_of(slot_g.at[q, k, 0], keep_w.at[q, k])
            all_of(m_g.at[k, layer, :, cols], keep_m.at[q, k])
            all_of(v_g.at[k, layer, :, cols], keep_v.at[q, k])
        return carry

    lax.fori_loop(0, layers * STRIPS, finish, 0)
    for r in range(layers):
        layer = top - r
        if r == layers - 1:
            dpair_copy(r).wait_send()
        for k in range(2):
            part = pl.ds(k * half, half)
            all_of(slot_d.at[r, k, pl.ds(0, chips - 1)], drs_send.at[r, k])
            all_of(slot_d.at[r, k, pl.ds(0, chips - 1)], dag_send.at[r, k])
            all_of(slot_d.at[r, k], dfw_send.at[r, k])
            all_of(slot_d.at[r, k], dfw_got.at[r, k])
            all_of(slot_d.at[r, k, 0], dkeep_w.at[r, k])
            all_of(m_d.at[layer, part], dkeep_m.at[r, k])
            all_of(v_d.at[layer, part], dkeep_v.at[r, k])


def solution(mesh):
    n = mesh.shape["dp"]

    def body(x, dy, wg, wu, wd, mg, mu, md, vg, vu, vd):
        x, dy = x[0], dy[0]
        tokens, d = x.shape
        layers, _, ff = wg.shape
        chips, rows, drows = n // 2, d // n, ff // n
        half, width = drows // 2, ff // STRIPS
        by_rows = pl.BlockSpec((BLOCK, d), lambda t: (t, 0))
        by_cols = pl.BlockSpec((d, BLOCK), lambda t: (0, t))
        tall, flat = jax.ShapeDtypeStruct((tokens, d), BF), jax.ShapeDtypeStruct((d, tokens), BF)
        up_spec = pl.BlockSpec((None, d, ff), lambda t: (0, 0, 0))
        down_spec = pl.BlockSpec((None, ff, d), lambda t: (0, 0, 0))
        a, at, h, b, bt, dyt = pl.pallas_call(
            forward,
            grid=(tokens // BLOCK,),
            in_specs=[by_rows, by_rows, up_spec, up_spec, down_spec],
            out_specs=[by_rows, by_cols, by_rows, by_rows, by_cols, by_cols],
            out_shape=[tall, flat, tall, tall, flat, flat],
            scratch_shapes=[pltpu.VMEM((BLOCK, ff), BF)],
            compiler_params=pltpu.CompilerParams(vmem_limit_bytes=60 * 2**20),
            name="forward",
        )(x, dy, wg, wu, wd)

        sds = jax.ShapeDtypeStruct
        vm, sem = pltpu.VMEM, pltpu.SemaphoreType.DMA
        q, r = layers * STRIPS, layers
        scratch = [
            vm((tokens, d), BF), vm((d, tokens), BF), vm((tokens, d), BF), vm((d, tokens), BF),
            vm((d, ff), BF), vm((d, ff), BF), vm((ff, d), BF),
            vm((2, tokens, ff), BF), vm((tokens, width), BF),
            vm((STRIPS, 2, 2, chips, rows, width), BF), vm((STRIPS, 2, chips, rows, width), BF),
            vm((layers, 2, chips, drows, d), BF), vm((chips, drows, d), BF),
            vm((q, 2, chips, rows, width), BF), vm((r, 2, chips, half, d), BF),
            vm((2, layers, rows, ff), BF), vm((layers, drows, d), BF),
            vm((2, layers, rows, ff), F32), vm((2, layers, rows, ff), F32),
            vm((layers, drows, d), F32), vm((layers, drows, d), F32),
            sem((7,)), sem((9,)), sem((q,)), sem((q,)),
            sem((q, 2)), sem((q, 2, chips - 1)), sem((q, 2)), sem((q, 2, chips - 1)), sem((q, 2)), sem((q, 2)),
            sem((q, 2)), sem((q, 2)), sem((q, 2)),
            sem((r,)), sem((r,)),
            sem((r, 2)), sem((r, 2, chips - 1)), sem((r, 2)), sem((r, 2, chips - 1)), sem((r, 2)), sem((r, 2)),
            sem((r, 2)), sem((r, 2)), sem((r, 2)),
            pltpu.SemaphoreType.REGULAR,
        ]
        return pl.pallas_call(
            functools.partial(backward, n),
            in_specs=[ANY] * 16,
            out_specs=[ANY] * 9,
            out_shape=[sds(t.shape, BF) for t in (wg, wu, wd)] + [sds(t.shape, F32) for t in (mg, mu, md, vg, vu, vd)],
            scratch_shapes=scratch,
            compiler_params=pltpu.CompilerParams(
                collective_id=0, has_side_effects=True, vmem_limit_bytes=67_043_328
            ),
            name="backward",
        )(b, bt, dy, dyt, h, a, at, wg, wu, wd, mg, mu, md, vg, vu, vd)

    seq, whole, rows = P(("rep", "dp"), None, None), P(None, None, None), P(None, "dp", None)
    return jax.shard_map(
        body,
        mesh=mesh,
        in_specs=(seq, seq, whole, whole, whole) + (rows,) * 6,
        out_specs=(P("rep", None, None),) * 3 + (P("rep", "dp", None),) * 6,
        check_vma=False,
    )
```

time: 711 us -> 276 us (0.39); the launches traced: 703 us -> 276 us
  waiting for transfers between devices: 421 us -> 0 us
  Pallas kernels: 0 us -> 259 us
  matrix products: 209 us -> 0 us
  other arithmetic: 32.5 us -> 0.01 us
  between operations: 14.9 us -> 0.7 us
  local copies, waits for them, and re-layouts: 24.6 us -> 16.2 us
    pallas_call x0 -> x2, Pallas kernels: none -> 259 us  [the longest x1 230 us: body(): pl.pallas_call(functools.partial(backward, n), in_specs=[ANY] * 16, out_s...]
    reduce_scatter x6 -> x0, waiting for transfers between devices: 215 us -> none  [body(): g = lax.psum_scatter(grads[n][name], 'dp', scatter_dimension=0, tiled=True)]
    dot_general x15 -> x0, matrix products: 209 us -> none  [the longest x5 79.1 us: layer(): gate = jnp.dot(a, w['w_gate'], preferred_element_type=jnp.float32)]
    all_gather x6 -> x0, waiting for transfers between devices: 204 us -> none  [body(): new[n, i] = (lax.all_gather(w1, 'dp', axis=0, tiled=True), m1, v1)]
    another operation x6 -> x0, other arithmetic: 22 us -> none  [body(): jnp.stack([new[n, i][k] for n in range(layers)])]
    slice x3 -> x0, local copies, waits for them, and re-layouts: 13.8 us -> none  [the longest x2 9.16 us: body(): w[n]]
    convert_element_type x3 -> x0, other arithmetic: 8.17 us -> none  [adamw(): return ((w - 0.02 * step).astype(jnp.bfloat16), m, v)]
    unnamed x36 -> x27, local copies, waits for them, and re-layouts: 10.8 us -> 16.2 us
  transfers between devices with their start and end apart: 12 -> 0, of which waited for: 10 -> 0; matrix products, arithmetic and copies ran while one was open for 21% -> 0% of each run, Pallas kernels for 0% -> 0%
where the time goes in v2:
time: 276 us
  Pallas kernels  259 us (94%)
  local copies, waits for them, and re-layouts  16.2 us (6%)
    pallas_call x1, Pallas kernels, body(): pl.pallas_call(functools.partial(backward, n), in_specs=[ANY] * 16, out_s...  230 us
    pallas_call x1, Pallas kernels, body(): pl.pallas_call(forward, grid=(tokens // BLOCK,), in_specs=[by_rows, by_ro...  29 us
    unnamed x27, local copies, waits for them, and re-layouts  16.2 us

profile of v2, /device:TPU:21, one launch (start us, length us, event | category | flops | bytes accessed | tf_op | source)
XLA Modules:
  0.0 275.9 jit_solution(14765280790354973586)
XLA Ops:
  0.6 29.0 %forward.1 = (bf16[2048,640]{1,0:T(8,128)(2,1)}, bf16[640,2048]{1,0:T(8,128)(2,1)}, bf16[2048,640]{1,0:T(8,128)(2,1)}, bf16[2048,640]{1,0:T(8,128)(2,1)}, bf16[6...) custom-call(bf16[2048,640]{1,0:T(8,128)(2,1)} %bitcast.6, bf16[2048,640]{1,0:T(8,128)(2,1)} %bitcast.2, ...), custom_call_target="tpu_custom_call" | custom-call | tf_op jit(solution)/shard_map/forward/pallas_call | solution.py:495
  29.6 230.1 %backward.1 = (bf16[2,640,2048]{2,1,0:T(8,128)(2,1)}, bf16[2,640,2048]{2,1,0:T(8,128)(2,1)}, bf16[2,2048,640]{2,1,0:T(8,128)(2,1)}, f32[2,40,2048]{2,1,0:T(8,128...) custom-call(bf16[2048,640]{1,0:T(8,128)(2,1)} %get-tuple-element.15., ...), custom_call_target="tpu_custom_call" | custom-call | tf_op jit(solution)/shard_map/backward/pallas_call | solution.py:527
  259.7 0.0 copy-start
  259.7 0.0 slice-start
  259.7 6.2 %copy.29 = bf16[2,640,2048]{2,1,0:T(8,128)(2,1)} copy(bf16[2,640,2048]{2,1,0:T(8,128)(2,1)} %get-tuple-element.30) | data formatting | bytes 10485760
  265.8 0.0 copy-done
  265.8 0.0 slice-start.1
  265.9 2.4 copy.30
  268.2 0.0 slice-done
  268.2 0.0 slice-done.1
  268.2 0.0 copy-start.6
  268.2 0.0 copy-start.5
  268.2 0.0 copy-start.4
  268.2 0.0 copy-start.3
  268.2 2.6 copy.31
  270.9 0.0 copy-done.6
  270.9 0.0 copy-start.2
  270.9 0.0 copy-start.1
  270.9 0.8 copy.32
  271.7 0.0 copy-done.5
  271.7 0.8 copy.33
  272.6 0.0 copy-done.4
  272.6 0.8 copy.34
  273.4 0.0 copy-done.3
  273.4 0.8 copy.35
  274.3 0.0 copy-done.2
  274.3 0.8 copy.36
  275.1 0.0 copy-done.1
  275.1 0.8 copy.37
  (1 shorter events, 0.0 us)
Async XLA Ops:
  259.7 6.2 %copy-start = (bf16[2,640,2048]{2,1,0:T(8,128)(2,1)S(1)}, bf16[2,640,2048]{2,1,0:T(8,128)(2,1)}, u32[]{:S(2)}) copy-start(bf16[2,640,2048]{2,1,0:T(8,128)(2,1)} %get-tuple-element.31) | copy-start | bytes 15728644
  259.7 8.5 %slice-start = ((s8[5242880]{0:T(1024)(128)(4,1)}), s8[4194304]{0:T(1024)(128)(4,1)S(1)}, s32[]{:S(2)}) async-start(s8[5242880]{0:T(1024)(128)(4,1)} %bitcast.4), calls=%async_computation | async-start | bytes 8388608
  265.8 2.4 slice-start.1
  268.2 2.7 copy-start.6
  268.2 3.5 %copy-start.5 = (f32[2,40,2048]{2,1,0:T(8,128)S(1)}, f32[2,40,2048]{2,1,0:T(8,128)}, u32[]{:S(2)}) copy-start(f32[2,40,2048]{2,1,0:T(8,128)} %get-tuple-element.34) | copy-start | bytes 1966084
  268.2 4.3 %copy-start.4 = (f32[2,128,640]{2,1,0:T(8,128)S(1)}, f32[2,128,640]{2,1,0:T(8,128)}, u32[]{:S(2)}) copy-start(f32[2,128,640]{2,1,0:T(8,128)} %get-tuple-element.35) | copy-start | bytes 1966084
  268.2 5.2 %copy-start.3 = (f32[2,40,2048]{2,1,0:T(8,128)S(1)}, f32[2,40,2048]{2,1,0:T(8,128)}, u32[]{:S(2)}) copy-start(f32[2,40,2048]{2,1,0:T(8,128)} %get-tuple-element.36) | copy-start | bytes 1966084
  270.9 3.4 %copy-start.2 = (f32[2,40,2048]{2,1,0:T(8,128)S(1)}, f32[2,40,2048]{2,1,0:T(8,128)}, u32[]{:S(2)}) copy-start(f32[2,40,2048]{2,1,0:T(8,128)} %get-tuple-element.37) | copy-start | bytes 1966084
  270.9 4.2 %copy-start.1 = (f32[2,128,640]{2,1,0:T(8,128)S(1)}, f32[2,128,640]{2,1,0:T(8,128)}, u32[]{:S(2)}) copy-start(f32[2,128,640]{2,1,0:T(8,128)} %get-tuple-element.38) | copy-start | bytes 1966084

commit v3 on v2

--- a/solution.py
+++ b/solution.py
@@ -57,8 +57,8 @@
     ng_ref, nu_ref, nd_ref, omg_ref, omu_ref, omd_ref, ovg_ref, ovu_ref, ovd_ref,
     act, actt, dy, dyt, wg, wu, wd, dgu, prod, own_g, got_g, own_d, got_d, slot_g, slot_d,
     wo_g, wo_d, m_g, v_g, m_d, v_d,
-    load, opt_load, pair_send, pair_got, rs_send, rs_got, ag_send, ag_got, fw_send, fw_got, keep_w, keep_m, keep_v,
-    dpair_send, dpair_got, drs_send, drs_got, dag_send, dag_got, dfw_send, dfw_got, dkeep_w, dkeep_m, dkeep_v, credit,
+    load, opt_load, pair_send, pair_got, rs_start, rs_send, rs_got, ag_send, ag_got, fw_send, fw_got, keep_w, keep_m, keep_v,
+    dpair_send, dpair_got, drs_start, drs_send, drs_got, dag_send, dag_got, dfw_send, dfw_got, dkeep_w, dkeep_m, dkeep_v, credit,
 ):
     chips = n // 2
     tokens, d = dy.shape
@@ -171,109 +171,135 @@
     def wrap(v):
         return lax.rem(v + 2 * chips, chips)
 
-    def hop(k, step):
-        return wrap(z - 1 - step) if k == 0 else wrap(z + 1 + step)
-
-    def ag_hop(k, step):
-        return wrap(z - step) if k == 0 else wrap(z + step)
+    far = chips // 2
+    ways = [((0, far - k, 0), (1, chips - 1 - (far - k), far - k)) for k in range(2)]
+
+    def coming(way, length, o):
+        return wrap(z + length - o) if way == 0 else wrap(z - length + o)
+
+    def going(way, s):
+        return wrap(z - s) if way == 0 else wrap(z + s)
 
     def ring_step(o, layer, j, q):
         for k in range(2):
-            b = hop(k, o)
-            mate_part = got_g[j, k, b].astype(F32) + own_g[j, c, k, b].astype(F32)
-
-            @pl.when(o == 0)
-            def _():
-                slot_g[q, k, chips - 1] = mate_part.astype(BF)
-                remote(slot_g.at[q, k, chips - 1], slot_g.at[q, k, 0], rs_send.at[q, k], rs_got.at[q, k, 0], near[k]).start()
-
-            @pl.when(o > 0)
-            def _():
-                here = slot_g.at[q, k, o - 1]
-                pltpu.make_async_copy(here, here, rs_got.at[q, k, o - 1]).wait()
-                here[...] = (here[...].astype(F32) + mate_part).astype(BF)
-                remote(here, slot_g.at[q, k, o], rs_send.at[q, k], rs_got.at[q, k, o], near[k]).start()
+            for way, length, base in ways[k]:
+
+                @pl.when(o < length)
+                def _():
+                    b = coming(way, length, o)
+                    own = own_g.at[j, c, k, b]
+                    part = got_g[j, k, b].astype(F32) + own[...].astype(F32)
+
+                    @pl.when(o == 0)
+                    def _():
+                        own[...] = part.astype(BF)
+                        remote(own, slot_g.at[q, k, base], rs_start.at[q, k], rs_got.at[q, k, base], near[way]).start()
+
+                    @pl.when(o > 0)
+                    def _():
+                        here = slot_g.at[q, k, base + o - 1]
+                        pltpu.make_async_copy(here, here, rs_got.at[q, k, base + o - 1]).wait()
+                        here[...] = (here[...].astype(F32) + part).astype(BF)
+                        remote(here, slot_g.at[q, k, base + o], rs_send.at[q, k], rs_got.at[q, k, base + o], near[way]).start()
 
     def dring_step(o, layer, r):
         for k in range(2):
-            b = hop(k, o)
-            part = pl.ds(k * half, half)
-            mate_part = got_d[b, part].astype(F32) + own_d[r, c, b, part].astype(F32)
-
-            @pl.when(o == 0)
-            def _():
-                slot_d[r, k, chips - 1] = mate_part.astype(BF)
-                remote(slot_d.at[r, k, chips - 1], slot_d.at[r, k, 0], drs_send.at[r, k], drs_got.at[r, k, 0], near[k]).start()
-
-            @pl.when(o > 0)
-            def _():
-                here = slot_d.at[r, k, o - 1]
-                pltpu.make_async_copy(here, here, drs_got.at[r, k, o - 1]).wait()
-                here[...] = (here[...].astype(F32) + mate_part).astype(BF)
-                remote(here, slot_d.at[r, k, o], drs_send.at[r, k], drs_got.at[r, k, o], near[k]).start()
-
-    def publish(src, dst, keep, send, got, fsend, fgot, to):
+            rows_k = pl.ds(k * half, half)
+            for way, length, base in ways[k]:
+
+                @pl.when(o < length)
+                def _():
+                    b = coming(way, length, o)
+                    own = own_d.at[r, c, b, rows_k]
+                    part = got_d[b, rows_k].astype(F32) + own[...].astype(F32)
+
+                    @pl.when(o == 0)
+                    def _():
+                        own[...] = part.astype(BF)
+                        remote(own, slot_d.at[r, k, base], drs_start.at[r, k], drs_got.at[r, k, base], near[way]).start()
+
+                    @pl.when(o > 0)
+                    def _():
+                        here = slot_d.at[r, k, base + o - 1]
+                        pltpu.make_async_copy(here, here, drs_got.at[r, k, base + o - 1]).wait()
+                        here[...] = (here[...].astype(F32) + part).astype(BF)
+                        remote(here, slot_d.at[r, k, base + o], drs_send.at[r, k], drs_got.at[r, k, base + o], near[way]).start()
+
+    def publish(src, dst, keep, send, got, fsend, fgot, k):
         pltpu.make_async_copy(src, dst, keep).start()
-        remote(src, dst, send, got, to).start()
+        for way, _, base in ways[k]:
+            remote(src, dst, send, got.at[base], near[way]).start()
         remote(src, dst, fsend, fgot, mate).start()
+
+    def arrived(slots, sems, starts, starting, k):
+        pltpu.make_async_copy(starting, starting, starts).wait()
+        first, second = (slots.at[base + length - 1] for _, length, base in ways[k])
+        for (_, length, base), here in zip(ways[k], (first, second)):
+            pltpu.make_async_copy(here, here, sems.at[base + length - 1]).wait()
+        return first, first[...].astype(F32) + second[...].astype(F32)
 
     def own_step(layer, j, q):
         cols, outs = strip_outs(layer, j)
         for k in range(2):
-            here = slot_g.at[q, k, chips - 2]
-            pltpu.make_async_copy(here, here, rs_got.at[q, k, chips - 2]).wait()
-            mate_part = got_g[j, k, z].astype(F32) + own_g[j, c, k, z].astype(F32)
-            g = (here[...].astype(F32) + mate_part).astype(BF).astype(F32)
+            here, sums = arrived(slot_g.at[q, k], rs_got.at[q, k], rs_start.at[q, k], own_g.at[j, c, k, pl.ds(0, 2)], k)
+            part = got_g[j, k, z].astype(F32) + own_g[j, c, k, z].astype(F32)
+            g = (sums + part).astype(BF).astype(F32)
             w1, m1, v1 = adamw(wo_g[k, layer, :, cols].astype(F32), m_g[k, layer, :, cols], v_g[k, layer, :, cols], g)
             m_g[k, layer, :, cols], v_g[k, layer, :, cols], here[...] = m1, v1, w1
+            publish(
+                here, outs[k].at[layer, block_of(k, z), cols], keep_w.at[q, k],
+                ag_send.at[q, k], ag_got.at[q, k], fw_send.at[q, k], fw_got.at[q, k], k,
+            )
             pltpu.make_async_copy(m_g.at[k, layer, :, cols], (omg_ref, omu_ref)[k].at[layer, :, cols], keep_m.at[q, k]).start()
             pltpu.make_async_copy(v_g.at[k, layer, :, cols], (ovg_ref, ovu_ref)[k].at[layer, :, cols], keep_v.at[q, k]).start()
-            publish(
-                here, outs[k].at[layer, block_of(k, z), cols], keep_w.at[q, k],
-                ag_send.at[q, k], ag_got.at[q, k, 0], fw_send.at[q, k], fw_got.at[q, k], near[k],
-            )
 
     def down_own_step(layer, r):
         for k in range(2):
-            part = pl.ds(k * half, half)
-            here = slot_d.at[r, k, chips - 2]
-            pltpu.make_async_copy(here, here, drs_got.at[r, k, chips - 2]).wait()
-            mate_part = got_d[z, part].astype(F32) + own_d[r, c, z, part].astype(F32)
-            g = (here[...].astype(F32) + mate_part).astype(BF).astype(F32)
-            w1, m1, v1 = adamw(wo_d[layer, part].astype(F32), m_d[layer, part], v_d[layer, part], g)
-            m_d[layer, part], v_d[layer, part], here[...] = m1, v1, w1
-            pltpu.make_async_copy(m_d.at[layer, part], omd_ref.at[layer, part], dkeep_m.at[r, k]).start()
-            pltpu.make_async_copy(v_d.at[layer, part], ovd_ref.at[layer, part], dkeep_v.at[r, k]).start()
+            rows_k = pl.ds(k * half, half)
+            starting = own_d.at[r, c, pl.ds(0, 2), rows_k]
+            here, sums = arrived(slot_d.at[r, k], drs_got.at[r, k], drs_start.at[r, k], starting, k)
+            part = got_d[z, rows_k].astype(F32) + own_d[r, c, z, rows_k].astype(F32)
+            g = (sums + part).astype(BF).astype(F32)
+            w1, m1, v1 = adamw(wo_d[layer, rows_k].astype(F32), m_d[layer, rows_k], v_d[layer, rows_k], g)
+            m_d[layer, rows_k], v_d[layer, rows_k], here[...] = m1, v1, w1
             publish(
                 here, nd_ref.at[layer, dblock_of(k, z)], dkeep_w.at[r, k],
-                dag_send.at[r, k], dag_got.at[r, k, 0], dfw_send.at[r, k], dfw_got.at[r, k], near[k],
+                dag_send.at[r, k], dag_got.at[r, k], dfw_send.at[r, k], dfw_got.at[r, k], k,
             )
+            pltpu.make_async_copy(m_d.at[layer, rows_k], omd_ref.at[layer, rows_k], dkeep_m.at[r, k]).start()
+            pltpu.make_async_copy(v_d.at[layer, rows_k], ovd_ref.at[layer, rows_k], dkeep_v.at[r, k]).start()
+
+    def hand_on(s, here_of, send, got, fsend, fgot, k):
+        for way, length, base in ways[k]:
+
+            @pl.when(s <= length)
+            def _():
+                here = here_of(going(way, s))
+                pltpu.make_async_copy(here, here, got.at[base + s - 1]).wait()
+
+                @pl.when(s < length)
+                def _():
+                    remote(here, here, send, got.at[base + s], near[way]).start()
+
+                remote(here, here, fsend, fgot, mate).start()
 
     def gather_step(s, layer, j, q):
         cols, outs = strip_outs(layer, j)
         for k in range(2):
-            here = outs[k].at[layer, block_of(k, ag_hop(k, s)), cols]
-            pltpu.make_async_copy(here, here, ag_got.at[q, k, s - 1]).wait()
-
-            @pl.when(s < chips - 1)
-            def _():
-                remote(here, here, ag_send.at[q, k], ag_got.at[q, k, s], near[k]).start()
-
-            remote(here, here, fw_send.at[q, k], fw_got.at[q, k], mate).start()
+            hand_on(
+                s, lambda b: outs[k].at[layer, block_of(k, b), cols],
+                ag_send.at[q, k], ag_got.at[q, k], fw_send.at[q, k], fw_got.at[q, k], k,
+            )
 
     def down_gather_step(s, layer, r):
         for k in range(2):
-            here = nd_ref.at[layer, dblock_of(k, ag_hop(k, s))]
-            pltpu.make_async_copy(here, here, dag_got.at[r, k, s - 1]).wait()
-
-            @pl.when(s < chips - 1)
-            def _():
-                remote(here, here, dag_send.at[r, k], dag_got.at[r, k, s], near[k]).start()
-
-            remote(here, here, dfw_send.at[r, k], dfw_got.at[r, k], mate).start()
-
-    steps = 2 * chips - 1
-    lags = steps // POINTS
+            hand_on(
+                s, lambda b: nd_ref.at[layer, dblock_of(k, b)],
+                dag_send.at[r, k], dag_got.at[r, k], dfw_send.at[r, k], dfw_got.at[r, k], k,
+            )
+
+    steps = 2 * far + 1
+    lags = -(-steps // POINTS)
 
     def point(i, p):
         def lag_step(idx, carry):
@@ -289,11 +315,11 @@
                 def _():
                     pltpu.make_async_copy(got_g.at[j], got_g.at[j], pair_got.at[q]).wait()
 
-                @pl.when(o < chips - 1)
+                @pl.when(o < far)
                 def _():
                     ring_step(o, layer, j, q)
 
-                @pl.when(o == chips - 1)
+                @pl.when(o == far)
                 def _():
                     @pl.when(g == 0)
                     def _():
@@ -302,9 +328,9 @@
 
                     own_step(layer, j, q)
 
-                @pl.when(o > chips - 1)
-                def _():
-                    gather_step(o - (chips - 1), layer, j, q)
+                @pl.when(o > far)
+                def _():
+                    gather_step(o - far, layer, j, q)
 
                 @pl.when(j == STRIPS - 1)
                 def _():
@@ -312,19 +338,19 @@
                     def _():
                         pltpu.make_async_copy(got_d, got_d, dpair_got.at[r]).wait()
 
-                    @pl.when(o < chips - 1)
+                    @pl.when(o < far)
                     def _():
                         dring_step(o, layer, r)
 
-                    @pl.when(o == chips - 1)
+                    @pl.when(o == far)
                     def _():
                         down_own_step(layer, r)
 
-                    @pl.when(o > chips - 1)
-                    def _():
-                        down_gather_step(o - (chips - 1), layer, r)
-
-                @pl.when((o == chips - 1) & (r < layers - 1))
+                    @pl.when(o > far)
+                    def _():
+                        down_gather_step(o - far, layer, r)
+
+                @pl.when((o == far) & (r < layers - 1))
                 def _():
                     pl.semaphore_signal(credit, inc=1, device_id={"dp": mate}, device_id_type=MESH)
 
@@ -453,10 +479,10 @@
             pair_copy(j, q).wait_send()
 
         for k in range(2):
-            all_of(slot_g.at[q, k, pl.ds(0, chips - 1)], rs_send.at[q, k])
+            all_of(slot_g.at[q, k, pl.ds(0, chips - 3)], rs_send.at[q, k])
             all_of(slot_g.at[q, k, pl.ds(0, chips - 1)], ag_send.at[q, k])
-            all_of(slot_g.at[q, k], fw_send.at[q, k])
-            all_of(slot_g.at[q, k], fw_got.at[q, k])
+            all_of(got_g.at[j, k], fw_send.at[q, k])
+            all_of(got_g.at[j, k], fw_got.at[q, k])
             all_of(slot_g.at[q, k, 0], keep_w.at[q, k])
             all_of(m_g.at[k, layer, :, cols], keep_m.at[q, k])
             all_of(v_g.at[k, layer, :, cols], keep_v.at[q, k])
@@ -469,10 +495,10 @@
             dpair_copy(r).wait_send()
         for k in range(2):
             part = pl.ds(k * half, half)
-            all_of(slot_d.at[r, k, pl.ds(0, chips - 1)], drs_send.at[r, k])
+            all_of(slot_d.at[r, k, pl.ds(0, chips - 3)], drs_send.at[r, k])
             all_of(slot_d.at[r, k, pl.ds(0, chips - 1)], dag_send.at[r, k])
-            all_of(slot_d.at[r, k], dfw_send.at[r, k])
-            all_of(slot_d.at[r, k], dfw_got.at[r, k])
+            all_of(got_d.at[:, part], dfw_send.at[r, k])
+            all_of(got_d.at[:, part], dfw_got.at[r, k])
             all_of(slot_d.at[r, k, 0], dkeep_w.at[r, k])
             all_of(m_d.at[layer, part], dkeep_m.at[r, k])
             all_of(v_d.at[layer, part], dkeep_v.at[r, k])
@@ -512,15 +538,15 @@
             vm((2, tokens, ff), BF), vm((tokens, width), BF),
             vm((STRIPS, 2, 2, chips, rows, width), BF), vm((STRIPS, 2, chips, rows, width), BF),
             vm((layers, 2, chips, drows, d), BF), vm((chips, drows, d), BF),
-            vm((q, 2, chips, rows, width), BF), vm((r, 2, chips, half, d), BF),
+            vm((q, 2, chips - 1, rows, width), BF), vm((r, 2, chips - 1, half, d), BF),
             vm((2, layers, rows, ff), BF), vm((layers, drows, d), BF),
             vm((2, layers, rows, ff), F32), vm((2, layers, rows, ff), F32),
             vm((layers, drows, d), F32), vm((layers, drows, d), F32),
             sem((7,)), sem((9,)), sem((q,)), sem((q,)),
-            sem((q, 2)), sem((q, 2, chips - 1)), sem((q, 2)), sem((q, 2, chips - 1)), sem((q, 2)), sem((q, 2)),
+            sem((q, 2)), sem((q, 2)), sem((q, 2, chips - 1)), sem((q, 2)), sem((q, 2, chips - 1)), sem((q, 2)), sem((q, 2)),
             sem((q, 2)), sem((q, 2)), sem((q, 2)),
             sem((r,)), sem((r,)),
-            sem((r, 2)), sem((r, 2, chips - 1)), sem((r, 2)), sem((r, 2, chips - 1)), sem((r, 2)), sem((r, 2)),
+            sem((r, 2)), sem((r, 2)), sem((r, 2, chips - 1)), sem((r, 2)), sem((r, 2, chips - 1)), sem((r, 2)), sem((r, 2)),
             sem((r, 2)), sem((r, 2)), sem((r, 2)),
             pltpu.SemaphoreType.REGULAR,
         ]

time: 276 us -> 266 us (0.964)
  Pallas kernels: 259 us -> 249 us
    pallas_call x1, Pallas kernels: 230 us -> 220 us  [body(): pl.pallas_call(functools.partial(backward, n), in_specs=[ANY] * 16, out_s...]
where the time goes in v3:
time: 266 us
  Pallas kernels  249 us (94%)
  local copies, waits for them, and re-layouts  16.2 us (6%)
    pallas_call x1, Pallas kernels, body(): pl.pallas_call(functools.partial(backward, n), in_specs=[ANY] * 16, out_s...  220 us
    pallas_call x1, Pallas kernels, body(): pl.pallas_call(forward, grid=(tokens // BLOCK,), in_specs=[by_rows, by_ro...  29 us
    unnamed x27, local copies, waits for them, and re-layouts  16.2 us

profile of v3, /device:TPU:21, one launch (start us, length us, event | category | flops | bytes accessed | tf_op | source)
XLA Modules:
  0.0 266.4 jit_solution(3361593286597787081)
XLA Ops:
  0.6 29.0 %forward.1 = (bf16[2048,640]{1,0:T(8,128)(2,1)}, bf16[640,2048]{1,0:T(8,128)(2,1)}, bf16[2048,640]{1,0:T(8,128)(2,1)}, bf16[2048,640]{1,0:T(8,128)(2,1)}, bf16[6...) custom-call(bf16[2048,640]{1,0:T(8,128)(2,1)} %bitcast.6, bf16[2048,640]{1,0:T(8,128)(2,1)} %bitcast.2, ...), custom_call_target="tpu_custom_call" | custom-call | tf_op jit(solution)/shard_map/forward/pallas_call | solution.py:521
  29.6 220.5 %backward.1 = (bf16[2,640,2048]{2,1,0:T(8,128)(2,1)}, bf16[2,640,2048]{2,1,0:T(8,128)(2,1)}, bf16[2,2048,640]{2,1,0:T(8,128)(2,1)}, f32[2,40,2048]{2,1,0:T(8,128...) custom-call(bf16[2048,640]{1,0:T(8,128)(2,1)} %get-tuple-element.15., ...), custom_call_target="tpu_custom_call" | custom-call | tf_op jit(solution)/shard_map/backward/pallas_call | solution.py:553
  250.1 0.0 copy-start
  250.1 0.0 slice-start
  250.1 6.2 %copy.29 = bf16[2,640,2048]{2,1,0:T(8,128)(2,1)} copy(bf16[2,640,2048]{2,1,0:T(8,128)(2,1)} %get-tuple-element.30) | data formatting | bytes 10485760
  256.3 0.0 copy-done
  256.3 0.0 slice-start.1
  256.3 2.4 copy.30
  258.7 0.0 slice-done
  258.7 0.0 slice-done.1
  258.7 0.0 copy-start.6
  258.7 0.0 copy-start.5
  258.7 0.0 copy-start.4
  258.7 0.0 copy-start.3
  258.7 2.6 copy.31
  261.3 0.0 copy-done.6
  261.3 0.0 copy-start.2
  261.3 0.0 copy-start.1
  261.3 0.8 copy.32
  262.2 0.0 copy-done.5
  262.2 0.8 copy.33
  263.0 0.0 copy-done.4
  263.0 0.8 copy.34
  263.9 0.0 copy-done.3
  263.9 0.8 copy.35
  264.7 0.0 copy-done.2
  264.7 0.8 copy.36
  265.5 0.0 copy-done.1
  265.5 0.8 copy.37
  (1 shorter events, 0.0 us)
Async XLA Ops:
  250.1 6.2 %copy-start = (bf16[2,640,2048]{2,1,0:T(8,128)(2,1)S(1)}, bf16[2,640,2048]{2,1,0:T(8,128)(2,1)}, u32[]{:S(2)}) copy-start(bf16[2,640,2048]{2,1,0:T(8,128)(2,1)} %get-tuple-element.31) | copy-start | bytes 15728644
  250.1 8.5 %slice-start = ((s8[5242880]{0:T(1024)(128)(4,1)}), s8[4194304]{0:T(1024)(128)(4,1)S(1)}, s32[]{:S(2)}) async-start(s8[5242880]{0:T(1024)(128)(4,1)} %bitcast.4), calls=%async_computation | async-start | bytes 8388608
  256.3 2.4 slice-start.1
  258.7 2.7 %copy-start.6 = (f32[2,40,2048]{2,1,0:T(8,128)S(1)}, f32[2,40,2048]{2,1,0:T(8,128)}, u32[]{:S(2)}) copy-start(f32[2,40,2048]{2,1,0:T(8,128)} %get-tuple-element.33) | copy-start | bytes 1966084
  258.7 3.5 %copy-start.5 = (f32[2,40,2048]{2,1,0:T(8,128)S(1)}, f32[2,40,2048]{2,1,0:T(8,128)}, u32[]{:S(2)}) copy-start(f32[2,40,2048]{2,1,0:T(8,128)} %get-tuple-element.34) | copy-start | bytes 1966084
  258.7 4.3 %copy-start.4 = (f32[2,128,640]{2,1,0:T(8,128)S(1)}, f32[2,128,640]{2,1,0:T(8,128)}, u32[]{:S(2)}) copy-start(f32[2,128,640]{2,1,0:T(8,128)} %get-tuple-element.35) | copy-start | bytes 1966084
  258.7 5.2 %copy-start.3 = (f32[2,40,2048]{2,1,0:T(8,128)S(1)}, f32[2,40,2048]{2,1,0:T(8,128)}, u32[]{:S(2)}) copy-start(f32[2,40,2048]{2,1,0:T(8,128)} %get-tuple-element.36) | copy-start | bytes 1966084
  261.3 3.4 %copy-start.2 = (f32[2,40,2048]{2,1,0:T(8,128)S(1)}, f32[2,40,2048]{2,1,0:T(8,128)}, u32[]{:S(2)}) copy-start(f32[2,40,2048]{2,1,0:T(8,128)} %get-tuple-element.37) | copy-start | bytes 1966084
  261.3 4.2 %copy-start.1 = (f32[2,128,640]{2,1,0:T(8,128)S(1)}, f32[2,128,640]{2,1,0:T(8,128)}, u32[]{:S(2)}) copy-start(f32[2,128,640]{2,1,0:T(8,128)} %get-tuple-element.38) | copy-start | bytes 1966084

commit v4 on v3

--- a/solution.py
+++ b/solution.py
@@ -9,9 +9,10 @@
 
 MESH = pl.DeviceIdType.MESH
 BF, F32 = jnp.bfloat16, jnp.float32
-BLOCK = 256
+BLOCK = 512
+TALL = 1024
 STRIPS = 4
-POINTS = 3
+POINTS = 6
 ANY = pl.BlockSpec(memory_space=pl.ANY)
 
 
@@ -115,28 +116,31 @@
     def tok(t):
         return pl.ds(pl.multiple_of(t * BLOCK, BLOCK), BLOCK)
 
-    def strip_block(j, t):
-        cols = pl.ds(pl.multiple_of(j * width, width), width)
-        a = act[tok(t), :]
+    pieces = width // 256
+    slabs = tokens // TALL * pieces
+
+    def strip_block(j, e):
+        rows_e = pl.ds(pl.multiple_of(e // pieces * TALL, TALL), TALL)
+        cols = pl.ds(pl.multiple_of(j * width + e % pieces * 256, 256), 256)
+        here = pl.ds(pl.multiple_of(e % pieces * 256, 256), 256)
+        a = act[rows_e, :]
         gate = dot(a, wg[:, cols])
         up = dot(a, wu[:, cols])
-        dact = dot(dy[tok(t), :], wd[cols, :], ((1,), (1,))).astype(BF).astype(F32)
+        dact = dot(dy[rows_e, :], wd[cols, :], ((1,), (1,))).astype(BF).astype(F32)
         sig = jax.nn.sigmoid(gate)
         silu = gate * sig
-        prod[tok(t), :] = (silu * up).astype(BF)
-        dgu[0, tok(t), cols] = (dact * up * (sig + silu * (1.0 - sig))).astype(BF)
-        dgu[1, tok(t), cols] = (dact * silu).astype(BF)
-
-    pieces = width // 256
-
-    def weight_rows(j, k, piece):
+        prod[rows_e, here] = (silu * up).astype(BF)
+        dgu[0, rows_e, cols] = (dact * up * (sig + silu * (1.0 - sig))).astype(BF)
+        dgu[1, rows_e, cols] = (dact * silu).astype(BF)
+
+    def weight_rows(q, j, k, piece):
         cols = pl.ds(pl.multiple_of(j * width + piece * 256, 256), 256)
         out = pl.ds(pl.multiple_of(piece * 256, 256), 256)
         total = dot(actt[...], dgu[k, :, cols])
         for chip in range(chips):
             for core in range(2):
                 at = (chip * 2 + core) * rows
-                own_g[j, core, k, chip, :, out] = total[at : at + rows].astype(BF)
+                own_g[jnp.where(c == core, j, STRIPS + q % 2), k, chip, :, out] = total[at : at + rows].astype(BF)
 
     def down_rows(r, j, piece):
         total = dot(dyt[...], prod[:, pl.ds(pl.multiple_of(piece * 256, 256), 256)])
@@ -145,7 +149,7 @@
         for k in range(per):
             for core in range(2):
                 at = (k * 2 + core) * drows
-                own_d[r, core, (j * pieces + piece) * per + k] = total[at : at + drows]
+                own_d[jnp.where(c == core, r, layers), (j * pieces + piece) * per + k] = total[at : at + drows]
 
     def state_block(t):
         by_gate = dot(dgu[0, tok(t), :], wg[...], ((1,), (1,))).astype(BF)
@@ -180,50 +184,48 @@
     def going(way, s):
         return wrap(z - s) if way == 0 else wrap(z + s)
 
-    def ring_step(o, layer, j, q):
-        for k in range(2):
-            for way, length, base in ways[k]:
-
-                @pl.when(o < length)
-                def _():
-                    b = coming(way, length, o)
-                    own = own_g.at[j, c, k, b]
-                    part = got_g[j, k, b].astype(F32) + own[...].astype(F32)
-
-                    @pl.when(o == 0)
-                    def _():
-                        own[...] = part.astype(BF)
-                        remote(own, slot_g.at[q, k, base], rs_start.at[q, k], rs_got.at[q, k, base], near[way]).start()
-
-                    @pl.when(o > 0)
-                    def _():
-                        here = slot_g.at[q, k, base + o - 1]
-                        pltpu.make_async_copy(here, here, rs_got.at[q, k, base + o - 1]).wait()
-                        here[...] = (here[...].astype(F32) + part).astype(BF)
-                        remote(here, slot_g.at[q, k, base + o], rs_send.at[q, k], rs_got.at[q, k, base + o], near[way]).start()
-
-    def dring_step(o, layer, r):
-        for k in range(2):
-            rows_k = pl.ds(k * half, half)
-            for way, length, base in ways[k]:
-
-                @pl.when(o < length)
-                def _():
-                    b = coming(way, length, o)
-                    own = own_d.at[r, c, b, rows_k]
-                    part = got_d[b, rows_k].astype(F32) + own[...].astype(F32)
-
-                    @pl.when(o == 0)
-                    def _():
-                        own[...] = part.astype(BF)
-                        remote(own, slot_d.at[r, k, base], drs_start.at[r, k], drs_got.at[r, k, base], near[way]).start()
-
-                    @pl.when(o > 0)
-                    def _():
-                        here = slot_d.at[r, k, base + o - 1]
-                        pltpu.make_async_copy(here, here, drs_got.at[r, k, base + o - 1]).wait()
-                        here[...] = (here[...].astype(F32) + part).astype(BF)
-                        remote(here, slot_d.at[r, k, base + o], drs_send.at[r, k], drs_got.at[r, k, base + o], near[way]).start()
+    def ring_step(o, layer, j, q, k):
+        for way, length, base in ways[k]:
+
+            @pl.when(o < length)
+            def _():
+                b = coming(way, length, o)
+                own = own_g.at[j, k, b]
+                part = got_g[j, k, b].astype(F32) + own[...].astype(F32)
+
+                @pl.when(o == 0)
+                def _():
+                    own[...] = part.astype(BF)
+                    remote(own, slot_g.at[q, k, base], rs_start.at[q, k], rs_got.at[q, k, base], near[way]).start()
+
+                @pl.when(o > 0)
+                def _():
+                    here = slot_g.at[q, k, base + o - 1]
+                    pltpu.make_async_copy(here, here, rs_got.at[q, k, base + o - 1]).wait()
+                    here[...] = (here[...].astype(F32) + part).astype(BF)
+                    remote(here, slot_g.at[q, k, base + o], rs_send.at[q, k], rs_got.at[q, k, base + o], near[way]).start()
+
+    def dring_step(o, layer, r, k):
+        rows_k = pl.ds(k * half, half)
+        for way, length, base in ways[k]:
+
+            @pl.when(o < length)
+            def _():
+                b = coming(way, length, o)
+                own = own_d.at[r, b, rows_k]
+                part = got_d[b, rows_k].astype(F32) + own[...].astype(F32)
+
+                @pl.when(o == 0)
+                def _():
+                    own[...] = part.astype(BF)
+                    remote(own, slot_d.at[r, k, base], drs_start.at[r, k], drs_got.at[r, k, base], near[way]).start()
+
+                @pl.when(o > 0)
+                def _():
+                    here = slot_d.at[r, k, base + o - 1]
+                    pltpu.make_async_copy(here, here, drs_got.at[r, k, base + o - 1]).wait()
+                    here[...] = (here[...].astype(F32) + part).astype(BF)
+                    remote(here, slot_d.at[r, k, base + o], drs_send.at[r, k], drs_got.at[r, k, base + o], near[way]).start()
 
     def publish(src, dst, keep, send, got, fsend, fgot, k):
         pltpu.make_async_copy(src, dst, keep).start()
@@ -238,36 +240,34 @@
             pltpu.make_async_copy(here, here, sems.at[base + length - 1]).wait()
         return first, first[...].astype(F32) + second[...].astype(F32)
 
-    def own_step(layer, j, q):
+    def own_step(layer, j, q, k):
         cols, outs = strip_outs(layer, j)
-        for k in range(2):
-            here, sums = arrived(slot_g.at[q, k], rs_got.at[q, k], rs_start.at[q, k], own_g.at[j, c, k, pl.ds(0, 2)], k)
-            part = got_g[j, k, z].astype(F32) + own_g[j, c, k, z].astype(F32)
-            g = (sums + part).astype(BF).astype(F32)
-            w1, m1, v1 = adamw(wo_g[k, layer, :, cols].astype(F32), m_g[k, layer, :, cols], v_g[k, layer, :, cols], g)
-            m_g[k, layer, :, cols], v_g[k, layer, :, cols], here[...] = m1, v1, w1
-            publish(
-                here, outs[k].at[layer, block_of(k, z), cols], keep_w.at[q, k],
-                ag_send.at[q, k], ag_got.at[q, k], fw_send.at[q, k], fw_got.at[q, k], k,
-            )
-            pltpu.make_async_copy(m_g.at[k, layer, :, cols], (omg_ref, omu_ref)[k].at[layer, :, cols], keep_m.at[q, k]).start()
-            pltpu.make_async_copy(v_g.at[k, layer, :, cols], (ovg_ref, ovu_ref)[k].at[layer, :, cols], keep_v.at[q, k]).start()
-
-    def down_own_step(layer, r):
-        for k in range(2):
-            rows_k = pl.ds(k * half, half)
-            starting = own_d.at[r, c, pl.ds(0, 2), rows_k]
-            here, sums = arrived(slot_d.at[r, k], drs_got.at[r, k], drs_start.at[r, k], starting, k)
-            part = got_d[z, rows_k].astype(F32) + own_d[r, c, z, rows_k].astype(F32)
-            g = (sums + part).astype(BF).astype(F32)
-            w1, m1, v1 = adamw(wo_d[layer, rows_k].astype(F32), m_d[layer, rows_k], v_d[layer, rows_k], g)
-            m_d[layer, rows_k], v_d[layer, rows_k], here[...] = m1, v1, w1
-            publish(
-                here, nd_ref.at[layer, dblock_of(k, z)], dkeep_w.at[r, k],
-                dag_send.at[r, k], dag_got.at[r, k], dfw_send.at[r, k], dfw_got.at[r, k], k,
-            )
-            pltpu.make_async_copy(m_d.at[layer, rows_k], omd_ref.at[layer, rows_k], dkeep_m.at[r, k]).start()
-            pltpu.make_async_copy(v_d.at[layer, rows_k], ovd_ref.at[layer, rows_k], dkeep_v.at[r, k]).start()
+        here, sums = arrived(slot_g.at[q, k], rs_got.at[q, k], rs_start.at[q, k], own_g.at[j, k, pl.ds(0, 2)], k)
+        part = got_g[j, k, z].astype(F32) + own_g[j, k, z].astype(F32)
+        g = (sums + part).astype(BF).astype(F32)
+        w1, m1, v1 = adamw(wo_g[k, layer, :, cols].astype(F32), m_g[k, layer, :, cols], v_g[k, layer, :, cols], g)
+        m_g[k, layer, :, cols], v_g[k, layer, :, cols], here[...] = m1, v1, w1
+        publish(
+            here, outs[k].at[layer, block_of(k, z), cols], keep_w.at[q, k],
+            ag_send.at[q, k], ag_got.at[q, k], fw_send.at[q, k], fw_got.at[q, k], k,
+        )
+        pltpu.make_async_copy(m_g.at[k, layer, :, cols], (omg_ref, omu_ref)[k].at[layer, :, cols], keep_m.at[q, k]).start()
+        pltpu.make_async_copy(v_g.at[k, layer, :, cols], (ovg_ref, ovu_ref)[k].at[layer, :, cols], keep_v.at[q, k]).start()
+
+    def down_own_step(layer, r, k):
+        rows_k = pl.ds(k * half, half)
+        starting = own_d.at[r, pl.ds(0, 2), rows_k]
+        here, sums = arrived(slot_d.at[r, k], drs_got.at[r, k], drs_start.at[r, k], starting, k)
+        part = got_d[z, rows_k].astype(F32) + own_d[r, z, rows_k].astype(F32)
+        g = (sums + part).astype(BF).astype(F32)
+        w1, m1, v1 = adamw(wo_d[layer, rows_k].astype(F32), m_d[layer, rows_k], v_d[layer, rows_k], g)
+        m_d[layer, rows_k], v_d[layer, rows_k], here[...] = m1, v1, w1
+        publish(
+            here, nd_ref.at[layer, dblock_of(k, z)], dkeep_w.at[r, k],
+            dag_send.at[r, k], dag_got.at[r, k], dfw_send.at[r, k], dfw_got.at[r, k], k,
+        )
+        pltpu.make_async_copy(m_d.at[layer, rows_k], omd_ref.at[layer, rows_k], dkeep_m.at[r, k]).start()
+        pltpu.make_async_copy(v_d.at[layer, rows_k], ovd_ref.at[layer, rows_k], dkeep_v.at[r, k]).start()
 
     def hand_on(s, here_of, send, got, fsend, fgot, k):
         for way, length, base in ways[k]:
@@ -283,88 +283,94 @@
 
                 remote(here, here, fsend, fgot, mate).start()
 
-    def gather_step(s, layer, j, q):
+    def gather_step(s, layer, j, q, k):
         cols, outs = strip_outs(layer, j)
-        for k in range(2):
-            hand_on(
-                s, lambda b: outs[k].at[layer, block_of(k, b), cols],
-                ag_send.at[q, k], ag_got.at[q, k], fw_send.at[q, k], fw_got.at[q, k], k,
-            )
-
-    def down_gather_step(s, layer, r):
-        for k in range(2):
-            hand_on(
-                s, lambda b: nd_ref.at[layer, dblock_of(k, b)],
-                dag_send.at[r, k], dag_got.at[r, k], dfw_send.at[r, k], dfw_got.at[r, k], k,
-            )
+        hand_on(
+            s, lambda b: outs[k].at[layer, block_of(k, b), cols],
+            ag_send.at[q, k], ag_got.at[q, k], fw_send.at[q, k], fw_got.at[q, k], k,
+        )
+
+    def down_gather_step(s, layer, r, k):
+        hand_on(
+            s, lambda b: nd_ref.at[layer, dblock_of(k, b)],
+            dag_send.at[r, k], dag_got.at[r, k], dfw_send.at[r, k], dfw_got.at[r, k], k,
+        )
 
     steps = 2 * far + 1
-    lags = -(-steps // POINTS)
+    per = POINTS // 2
+    lags = -(-steps // per)
 
     def point(i, p):
-        def lag_step(idx, carry):
-            lag = lags - idx
+        def advance(lag, k):
             g = i - lag
             r, j = g // turns, g % turns
-            o = (lag - 1) * POINTS + p
+            o = (lag - 1) * per + p // 2
             layer, q = top - r, r * STRIPS + j
 
             @pl.when((g >= 0) & (g <= last) & (j < STRIPS))
             def _():
-                @pl.when(o == 0)
-                def _():
-                    pltpu.make_async_copy(got_g.at[j], got_g.at[j], pair_got.at[q]).wait()
-
-                @pl.when(o < far)
-                def _():
-                    ring_step(o, layer, j, q)
-
-                @pl.when(o == far)
-                def _():
-                    @pl.when(g == 0)
+                if k == 0:
+
+                    @pl.when(o == 0)
+                    def _():
+                        pltpu.make_async_copy(got_g.at[j], got_g.at[j], pair_got.at[q]).wait()
+
+                    @pl.when((o == 0) & (j == STRIPS - 1))
+                    def _():
+                        pltpu.make_async_copy(got_d, got_d, dpair_got.at[r]).wait()
+
+                    @pl.when((o == far) & (g == 0))
                     def _():
                         for copy in params:
                             copy.wait()
 
-                    own_step(layer, j, q)
+                @pl.when(o < far)
+                def _():
+                    ring_step(o, layer, j, q, k)
+
+                @pl.when(o == far)
+                def _():
+                    own_step(layer, j, q, k)
 
                 @pl.when(o > far)
                 def _():
-                    gather_step(o - far, layer, j, q)
+                    gather_step(o - far, layer, j, q, k)
 
                 @pl.when(j == STRIPS - 1)
                 def _():
-                    @pl.when(o == 0)
-                    def _():
-                        pltpu.make_async_copy(got_d, got_d, dpair_got.at[r]).wait()
-
                     @pl.when(o < far)
                     def _():
-                        dring_step(o, layer, r)
+                        dring_step(o, layer, r, k)
 
                     @pl.when(o == far)
                     def _():
-                        down_own_step(layer, r)
+                        down_own_step(layer, r, k)
 
                     @pl.when(o > far)
                     def _():
-                        down_gather_step(o - far, layer, r)
-
-                @pl.when((o == far) & (r < layers - 1))
-                def _():
-                    pl.semaphore_signal(credit, inc=1, device_id={"dp": mate}, device_id_type=MESH)
-
-            return carry
-
-        lax.fori_loop(0, lags, lag_step, 0)
+                        down_gather_step(o - far, layer, r, k)
+
+                if k == 1:
+
+                    @pl.when((o == far) & (r < layers - 1))
+                    def _():
+                        pl.semaphore_signal(credit, inc=1, device_id={"dp": mate}, device_id_type=MESH)
+
+        for k in range(2):
+
+            @pl.when(p % 2 == k)
+            def _():
+                def lag_step(idx, carry):
+                    advance(lags - idx, k)
+                    return carry
+
+                lax.fori_loop(0, lags, lag_step, 0)
 
     def pair_copy(j, q):
-        return remote(own_g.at[j, 1 - c], got_g.at[j], pair_send.at[q], pair_got.at[q], mate)
+        return remote(own_g.at[STRIPS + q % 2], got_g.at[j], pair_send.at[q], pair_got.at[q], mate)
 
     def dpair_copy(r):
-        return remote(own_d.at[r, 1 - c], got_d, dpair_send.at[r], dpair_got.at[r], mate)
-
-    cut = (0, blocks // 2, blocks)
+        return remote(own_d.at[layers], got_d, dpair_send.at[r], dpair_got.at[r], mate)
 
     def segment(i, p):
         r, j = i // turns, i % turns
@@ -381,44 +387,41 @@
             for k in range(4):
                 second[k].wait()
 
-        @pl.when(strip & (p < 2))
-        def _():
-            def one(t, carry):
-                strip_block(j, t)
-                return carry
-
-            lax.fori_loop(p * (blocks // 2), (p + 1) * (blocks // 2), one, 0)
-
-        @pl.when(strip & (p == 1))
-        def _():
-            @pl.when(i == STRIPS - 1)
-            def _():
-                states.start()
-
-        @pl.when((i == 0) & (p == 1))
+        @pl.when(strip & (p < slabs))
+        def _():
+            strip_block(j, p)
+
+        @pl.when((i == STRIPS - 1) & (p == slabs))
+        def _():
+            states.start()
+
+        @pl.when((i == 0) & (p == slabs - 1))
         def _():
             for k in (4, 6):
                 first[k].wait()
 
-        @pl.when((i == turns) & (p == 1))
+        @pl.when((i == turns) & (p == slabs - 1))
         def _():
             second[4].wait()
 
-        @pl.when(strip & (p == 1) & (r > 0))
-        def _():
-            pair_copy(j, q - STRIPS).wait_send()
-
-            @pl.when(j == 0)
+        @pl.when(strip & (p == slabs - 1))
+        def _():
+            @pl.when(q >= 2)
+            def _():
+                pair_copy(j, q - 2).wait_send()
+
+            @pl.when((r > 0) & (j == 0))
             def _():
                 dpair_copy(r - 1).wait_send()
 
-        @pl.when(strip & (p > 0))
+        @pl.when(strip & (p >= slabs - 1))
         def _():
             def one(e, carry):
-                weight_rows(j, e // pieces, e % pieces)
+                weight_rows(q, j, e // pieces, e % pieces)
                 return carry
 
-            lax.fori_loop((p - 1) * pieces, p * pieces, one, 0)
+            ahead = p - (slabs - 1)
+            lax.fori_loop(jnp.maximum(2 * ahead - 1, 0), jnp.minimum(2 * ahead + 1, 2 * pieces), one, 0)
 
         @pl.when(strip & (p == POINTS - 1))
         def _():
@@ -474,7 +477,7 @@
         layer = top - q // STRIPS
         cols, outs = strip_outs(layer, j)
 
-        @pl.when(q >= (layers - 1) * STRIPS)
+        @pl.when(q >= layers * STRIPS - 2)
         def _():
             pair_copy(j, q).wait_send()
 
@@ -536,8 +539,8 @@
             vm((tokens, d), BF), vm((d, tokens), BF), vm((tokens, d), BF), vm((d, tokens), BF),
             vm((d, ff), BF), vm((d, ff), BF), vm((ff, d), BF),
             vm((2, tokens, ff), BF), vm((tokens, width), BF),
-            vm((STRIPS, 2, 2, chips, rows, width), BF), vm((STRIPS, 2, chips, rows, width), BF),
-            vm((layers, 2, chips, drows, d), BF), vm((chips, drows, d), BF),
+            vm((STRIPS + 2, 2, chips, rows, width), BF), vm((STRIPS, 2, chips, rows, width), BF),
+            vm((layers + 1, chips, drows, d), BF), vm((chips, drows, d), BF),
             vm((q, 2, chips - 1, rows, width), BF), vm((r, 2, chips - 1, half, d), BF),
             vm((2, layers, rows, ff), BF), vm((layers, drows, d), BF),
             vm((2, layers, rows, ff), F32), vm((2, layers, rows, ff), F32),

time: 266 us -> 262 us (0.985)
  Pallas kernels: 249 us -> 245 us
    pallas_call x1, Pallas kernels: 220 us -> 217 us  [body(): pl.pallas_call(functools.partial(backward, n), in_specs=[ANY] * 16, out_s...]
where the time goes in v4:
time: 262 us
  Pallas kernels  245 us (94%)
  local copies, waits for them, and re-layouts  16.2 us (6%)
    pallas_call x1, Pallas kernels, body(): pl.pallas_call(functools.partial(backward, n), in_specs=[ANY] * 16, out_s...  217 us
    pallas_call x1, Pallas kernels, body(): pl.pallas_call(forward, grid=(tokens // BLOCK,), in_specs=[by_rows, by_ro...  27.9 us
    unnamed x27, local copies, waits for them, and re-layouts  16.2 us

profile of v4, /device:TPU:21, one launch (start us, length us, event | category | flops | bytes accessed | tf_op | source)
XLA Modules:
  0.0 262.2 jit_solution(2812219388191416975)
XLA Ops:
  0.6 27.9 %forward.1 = (bf16[2048,640]{1,0:T(8,128)(2,1)}, bf16[640,2048]{1,0:T(8,128)(2,1)}, bf16[2048,640]{1,0:T(8,128)(2,1)}, bf16[2048,640]{1,0:T(8,128)(2,1)}, bf16[6...) custom-call(bf16[2048,640]{1,0:T(8,128)(2,1)} %bitcast.6, bf16[2048,640]{1,0:T(8,128)(2,1)} %bitcast.2, ...), custom_call_target="tpu_custom_call" | custom-call | tf_op jit(solution)/shard_map/forward/pallas_call | solution.py:524
  28.5 217.4 %backward.1 = (bf16[2,640,2048]{2,1,0:T(8,128)(2,1)}, bf16[2,640,2048]{2,1,0:T(8,128)(2,1)}, bf16[2,2048,640]{2,1,0:T(8,128)(2,1)}, f32[2,40,2048]{2,1,0:T(8,128...) custom-call(bf16[2048,640]{1,0:T(8,128)(2,1)} %get-tuple-element.15., ...), custom_call_target="tpu_custom_call" | custom-call | tf_op jit(solution)/shard_map/backward/pallas_call | solution.py:556
  245.9 0.0 copy-start
  245.9 0.0 slice-start
  245.9 6.2 %copy.29 = bf16[2,640,2048]{2,1,0:T(8,128)(2,1)} copy(bf16[2,640,2048]{2,1,0:T(8,128)(2,1)} %get-tuple-element.30) | data formatting | bytes 10485760
  252.1 0.0 copy-done
  252.1 0.0 slice-start.1
  252.1 2.4 copy.30
  254.4 0.0 slice-done
  254.4 0.0 slice-done.1
  254.4 0.0 copy-start.6
  254.5 0.0 copy-start.5
  254.5 0.0 copy-start.4
  254.5 0.0 copy-start.3
  254.5 2.6 %copy.31 = bf16[2,2048,640]{2,1,0:T(8,128)(2,1)} copy(bf16[2,2048,640]{2,1,0:T(8,128)(2,1)S(1)} %bitcast.5) | data formatting | bytes 10485760
  257.1 0.0 copy-done.6
  257.1 0.0 copy-start.2
  257.1 0.0 copy-start.1
  257.1 0.8 copy.32
  258.0 0.0 copy-done.5
  258.0 0.8 copy.33
  258.8 0.0 copy-done.4
  258.8 0.8 copy.34
  259.7 0.0 copy-done.3
  259.7 0.8 copy.35
  260.5 0.0 copy-done.2
  260.5 0.8 copy.36
  261.3 0.0 copy-done.1
  261.3 0.8 copy.37
  (1 shorter events, 0.0 us)
Async XLA Ops:
  245.9 6.2 %copy-start = (bf16[2,640,2048]{2,1,0:T(8,128)(2,1)S(1)}, bf16[2,640,2048]{2,1,0:T(8,128)(2,1)}, u32[]{:S(2)}) copy-start(bf16[2,640,2048]{2,1,0:T(8,128)(2,1)} %get-tuple-element.31) | copy-start | bytes 15728644
  245.9 8.5 %slice-start = ((s8[5242880]{0:T(1024)(128)(4,1)}), s8[4194304]{0:T(1024)(128)(4,1)S(1)}, s32[]{:S(2)}) async-start(s8[5242880]{0:T(1024)(128)(4,1)} %bitcast.4), calls=%async_computation | async-start | bytes 8388608
  252.1 2.4 slice-start.1
  254.4 2.7 %copy-start.6 = (f32[2,40,2048]{2,1,0:T(8,128)S(1)}, f32[2,40,2048]{2,1,0:T(8,128)}, u32[]{:S(2)}) copy-start(f32[2,40,2048]{2,1,0:T(8,128)} %get-tuple-element.33) | copy-start | bytes 1966084
  254.5 3.5 %copy-start.5 = (f32[2,40,2048]{2,1,0:T(8,128)S(1)}, f32[2,40,2048]{2,1,0:T(8,128)}, u32[]{:S(2)}) copy-start(f32[2,40,2048]{2,1,0:T(8,128)} %get-tuple-element.34) | copy-start | bytes 1966084
  254.5 4.3 %copy-start.4 = (f32[2,128,640]{2,1,0:T(8,128)S(1)}, f32[2,128,640]{2,1,0:T(8,128)}, u32[]{:S(2)}) copy-start(f32[2,128,640]{2,1,0:T(8,128)} %get-tuple-element.35) | copy-start | bytes 1966084
  254.5 5.2 %copy-start.3 = (f32[2,40,2048]{2,1,0:T(8,128)S(1)}, f32[2,40,2048]{2,1,0:T(8,128)}, u32[]{:S(2)}) copy-start(f32[2,40,2048]{2,1,0:T(8,128)} %get-tuple-element.36) | copy-start | bytes 1966084
  257.1 3.4 %copy-start.2 = (f32[2,40,2048]{2,1,0:T(8,128)S(1)}, f32[2,40,2048]{2,1,0:T(8,128)}, u32[]{:S(2)}) copy-start(f32[2,40,2048]{2,1,0:T(8,128)} %get-tuple-element.37) | copy-start | bytes 1966084
  257.1 4.2 %copy-start.1 = (f32[2,128,640]{2,1,0:T(8,128)S(1)}, f32[2,128,640]{2,1,0:T(8,128)}, u32[]{:S(2)}) copy-start(f32[2,128,640]{2,1,0:T(8,128)} %get-tuple-element.38) | copy-start | bytes 1966084

commit v5 on v4

--- a/solution.py
+++ b/solution.py
@@ -24,27 +24,6 @@
     return lax.rsqrt(jnp.mean(wide * wide, -1, keepdims=True) + 1e-6)
 
 
-def forward(x_ref, dy_ref, wg_ref, wu_ref, wd_ref, a_ref, at_ref, h_ref, b_ref, bt_ref, dyt_ref, act_ref):
-    wide = x_ref[...].astype(F32)
-    a = wide * scale_of(wide)
-    at_ref[...] = a.T.astype(BF)
-    a = a.astype(BF)
-    a_ref[...] = a
-    width = wg_ref.shape[1] // STRIPS
-    for j in range(STRIPS):
-        cols = slice(j * width, (j + 1) * width)
-        gate, up = dot(a, wg_ref[:, cols]), dot(a, wu_ref[:, cols])
-        act_ref[:, cols] = (gate * jax.nn.sigmoid(gate) * up).astype(BF)
-    down = dot(act_ref[...], wd_ref[...]).astype(BF)
-    h = (wide + down.astype(F32)).astype(BF)
-    h_ref[...] = h
-    wide = h.astype(F32)
-    b = wide * scale_of(wide)
-    bt_ref[...] = b.T.astype(BF)
-    b_ref[...] = b.astype(BF)
-    dyt_ref[...] = dy_ref[...].astype(F32).T.astype(BF)
-
-
 def adamw(w, m, v, g):
     m = 0.9 * m + 0.1 * g
     v = 0.95 * v + 0.05 * g * g
@@ -52,13 +31,13 @@
     return (w - 0.02 * step).astype(BF), m, v
 
 
-def backward(
-    n, b_ref, bt_ref, dyi_ref, dyti_ref, h_ref, a_ref, at_ref, wg_ref, wu_ref, wd_ref,
+def train(
+    n, x_ref, dyi_ref, wg_ref, wu_ref, wd_ref,
     mg_ref, mu_ref, md_ref, vg_ref, vu_ref, vd_ref,
-    ng_ref, nu_ref, nd_ref, omg_ref, omu_ref, omd_ref, ovg_ref, ovu_ref, ovd_ref,
+    ng_ref, nu_ref, nd_ref, omg_ref, omu_ref, omd_ref, ovg_ref, ovu_ref, ovd_ref, h_ref, a_ref, at_ref,
     act, actt, dy, dyt, wg, wu, wd, dgu, prod, own_g, got_g, own_d, got_d, slot_g, slot_d,
     wo_g, wo_d, m_g, v_g, m_d, v_d,
-    load, opt_load, pair_send, pair_got, rs_start, rs_send, rs_got, ag_send, ag_got, fw_send, fw_got, keep_w, keep_m, keep_v,
+    load, x_load, first_out, opt_load, pair_send, pair_got, rs_start, rs_send, rs_got, ag_send, ag_got, fw_send, fw_got, keep_w, keep_m, keep_v,
     dpair_send, dpair_got, drs_start, drs_send, drs_got, dag_send, dag_got, dfw_send, dfw_got, dkeep_w, dkeep_m, dkeep_v, credit,
 ):
     chips = n // 2
@@ -87,15 +66,30 @@
 
     top = layers - 1
 
+    def tok(t):
+        return pl.ds(pl.multiple_of(t * BLOCK, BLOCK), BLOCK)
+
     def loads(layer, acts, actst):
         return (
             fetch(acts, act, 0), fetch(wg_ref.at[layer], wg, 1), fetch(wu_ref.at[layer], wu, 2),
             fetch(wd_ref.at[layer], wd, 3), fetch(actst, actt, 4),
         )
 
-    first = (*loads(top, b_ref, bt_ref), fetch(dyi_ref, dy, 5), fetch(dyti_ref, dyt, 6))
-    for k in (0, 1, 2, 5, 3, 4, 6):
-        first[k].start()
+    wg_v, wu_v, at_v = (dgu.at[0, pl.ds(k * d, d)] for k in range(3))
+    wd_v, x_v, h_v = (dgu.at[1, :, pl.ds(k * d, d)] for k in range(3))
+
+    def x_copy(t):
+        return pltpu.make_async_copy(x_ref.at[tok(t)], x_v.at[tok(t)], x_load.at[t])
+
+    early = (fetch(wg_ref.at[0], wg_v, 5), fetch(wu_ref.at[0], wu_v, 6), fetch(wd_ref.at[0], wd_v, 7), fetch(dyi_ref, dy, 8))
+    first = (None, fetch(wg_ref.at[top], wg, 1), fetch(wu_ref.at[top], wu, 2), fetch(wd_ref.at[top], wd, 3))
+    x_copy(0).start()
+    for copy in early:
+        copy.start()
+    for t in range(1, blocks):
+        x_copy(t).start()
+    for copy in first[1:]:
+        copy.start()
     mine = pl.ds(pl.multiple_of(me * rows, 8), rows)
     dmine = pl.ds(pl.multiple_of(me * drows, 8), drows)
     params = [
@@ -113,8 +107,54 @@
     def remote(src, dst, send, got, to):
         return pltpu.make_async_remote_copy(src, dst, send, got, device_id={"dp": to}, device_id_type=MESH)
 
-    def tok(t):
-        return pl.ds(pl.multiple_of(t * BLOCK, BLOCK), BLOCK)
+    def first_outs(part):
+        return (
+            pltpu.make_async_copy(x_v.at[part], a_ref.at[part], first_out.at[0]),
+            pltpu.make_async_copy(at_v.at[:, part], at_ref.at[:, part], first_out.at[1]),
+            pltpu.make_async_copy(h_v.at[part], h_ref.at[part], first_out.at[2]),
+        )
+
+    def forward_block(t):
+        x_copy(t).wait()
+        part = tok(t)
+        wide = x_v[part, :].astype(F32)
+        a = wide * scale_of(wide)
+        at_v[:, part] = a.T.astype(BF)
+        a = a.astype(BF)
+        for j in range(STRIPS):
+            cols = slice(j * width, (j + 1) * width)
+            gate, up = dot(a, wg_v[:, cols]), dot(a, wu_v[:, cols])
+            prod[j * BLOCK : (j + 1) * BLOCK, :] = (gate * jax.nn.sigmoid(gate) * up).astype(BF)
+
+        @pl.when(t == 0)
+        def _():
+            early[2].wait()
+            early[3].wait()
+
+        down = sum(
+            dot(prod[j * BLOCK : (j + 1) * BLOCK, :], wd_v[j * width : (j + 1) * width, :]) for j in range(STRIPS)
+        ).astype(BF)
+        h = (wide + down.astype(F32)).astype(BF)
+        x_v[part, :] = a
+        h_v[part, :] = h
+        wide = h.astype(F32)
+        b = wide * scale_of(wide)
+        actt[:, part] = b.T.astype(BF)
+        act[part, :] = b.astype(BF)
+        dyt[:, part] = dy[part, :].astype(F32).T.astype(BF)
+        for copy in first_outs(part):
+            copy.start()
+
+    early[0].wait()
+    early[1].wait()
+
+    def forward_step(t, carry):
+        forward_block(t)
+        return carry
+
+    lax.fori_loop(0, blocks, forward_step, 0)
+    for copy in first_outs(pl.ds(0, tokens)):
+        copy.wait()
 
     pieces = width // 256
     slabs = tokens // TALL * pieces
@@ -379,7 +419,7 @@
 
         @pl.when((i == 0) & (p == 0))
         def _():
-            for k in (0, 1, 2, 3, 5):
+            for k in (1, 2, 3):
                 first[k].wait()
 
         @pl.when((i == turns) & (p == 0))
@@ -394,11 +434,6 @@
         @pl.when((i == STRIPS - 1) & (p == slabs))
         def _():
             states.start()
-
-        @pl.when((i == 0) & (p == slabs - 1))
-        def _():
-            for k in (4, 6):
-                first[k].wait()
 
         @pl.when((i == turns) & (p == slabs - 1))
         def _():
@@ -425,17 +460,17 @@
 
         @pl.when(strip & (p == POINTS - 1))
         def _():
+            @pl.when(r > 0)
+            def _():
+                pl.semaphore_wait(credit, 1)
+
+            pair_copy(j, q).start()
+
             def one(e, carry):
                 down_rows(r, j, e)
                 return carry
 
             lax.fori_loop(0, pieces, one, 0)
-
-            @pl.when(r > 0)
-            def _():
-                pl.semaphore_wait(credit, 1)
-
-            pair_copy(j, q).start()
 
             @pl.when(j == STRIPS - 1)
             def _():
@@ -516,22 +551,7 @@
         layers, _, ff = wg.shape
         chips, rows, drows = n // 2, d // n, ff // n
         half, width = drows // 2, ff // STRIPS
-        by_rows = pl.BlockSpec((BLOCK, d), lambda t: (t, 0))
-        by_cols = pl.BlockSpec((d, BLOCK), lambda t: (0, t))
         tall, flat = jax.ShapeDtypeStruct((tokens, d), BF), jax.ShapeDtypeStruct((d, tokens), BF)
-        up_spec = pl.BlockSpec((None, d, ff), lambda t: (0, 0, 0))
-        down_spec = pl.BlockSpec((None, ff, d), lambda t: (0, 0, 0))
-        a, at, h, b, bt, dyt = pl.pallas_call(
-            forward,
-            grid=(tokens // BLOCK,),
-            in_specs=[by_rows, by_rows, up_spec, up_spec, down_spec],
-            out_specs=[by_rows, by_cols, by_rows, by_rows, by_cols, by_cols],
-            out_shape=[tall, flat, tall, tall, flat, flat],
-            scratch_shapes=[pltpu.VMEM((BLOCK, ff), BF)],
-            compiler_params=pltpu.CompilerParams(vmem_limit_bytes=60 * 2**20),
-            name="forward",
-        )(x, dy, wg, wu, wd)
-
         sds = jax.ShapeDtypeStruct
         vm, sem = pltpu.VMEM, pltpu.SemaphoreType.DMA
         q, r = layers * STRIPS, layers
@@ -545,7 +565,7 @@
             vm((2, layers, rows, ff), BF), vm((layers, drows, d), BF),
             vm((2, layers, rows, ff), F32), vm((2, layers, rows, ff), F32),
             vm((layers, drows, d), F32), vm((layers, drows, d), F32),
-            sem((7,)), sem((9,)), sem((q,)), sem((q,)),
+            sem((9,)), sem((tokens // BLOCK,)), sem((3,)), sem((9,)), sem((q,)), sem((q,)),
             sem((q, 2)), sem((q, 2)), sem((q, 2, chips - 1)), sem((q, 2)), sem((q, 2, chips - 1)), sem((q, 2)), sem((q, 2)),
             sem((q, 2)), sem((q, 2)), sem((q, 2)),
             sem((r,)), sem((r,)),
@@ -554,16 +574,16 @@
             pltpu.SemaphoreType.REGULAR,
         ]
         return pl.pallas_call(
-            functools.partial(backward, n),
-            in_specs=[ANY] * 16,
-            out_specs=[ANY] * 9,
-            out_shape=[sds(t.shape, BF) for t in (wg, wu, wd)] + [sds(t.shape, F32) for t in (mg, mu, md, vg, vu, vd)],
+            functools.partial(train, n),
+            in_specs=[ANY] * 11,
+            out_specs=[ANY] * 12,
+            out_shape=[sds(t.shape, BF) for t in (wg, wu, wd)] + [sds(t.shape, F32) for t in (mg, mu, md, vg, vu, vd)] + [tall, tall, flat],
             scratch_shapes=scratch,
             compiler_params=pltpu.CompilerParams(
                 collective_id=0, has_side_effects=True, vmem_limit_bytes=67_043_328
             ),
-            name="backward",
-        )(b, bt, dy, dyt, h, a, at, wg, wu, wd, mg, mu, md, vg, vu, vd)
+            name="step",
+        )(x, dy, wg, wu, wd, mg, mu, md, vg, vu, vd)[:9]
 
     seq, whole, rows = P(("rep", "dp"), None, None), P(None, None, None), P(None, "dp", None)
     return jax.shard_map(

time: 262 us -> 258 us (0.985)
  Pallas kernels: 245 us -> 241 us
    pallas_call x2 -> x1, Pallas kernels: 245 us -> 241 us  [body(): pl.pallas_call(functools.partial(train, n), in_specs=[ANY] * 11, out_spec...]
where the time goes in v5:
time: 258 us
  Pallas kernels  241 us (93%)
  local copies, waits for them, and re-layouts  16.2 us (6%)
    pallas_call x1, Pallas kernels, body(): pl.pallas_call(functools.partial(train, n), in_specs=[ANY] * 11, out_spec...  241 us
    unnamed x27, local copies, waits for them, and re-layouts  16.2 us

profile of v5, /device:TPU:21, one launch (start us, length us, event | category | flops | bytes accessed | tf_op | source)
XLA Modules:
  0.0 258.4 jit_solution(25736353898546370)
XLA Ops:
  0.6 241.5 %step.1 = (bf16[2,640,2048]{2,1,0:T(8,128)(2,1)}, bf16[2,640,2048]{2,1,0:T(8,128)(2,1)}, bf16[2,2048,640]{2,1,0:T(8,128)(2,1)}, f32[2,40,2048]{2,1,0:T(8,128)}, ...) custom-call(bf16[2048,640]{1,0:T(8,128)(2,1)} %bitcast.4, ...), custom_call_target="tpu_custom_call" | custom-call | tf_op jit(solution)/shard_map/step/pallas_call | solution.py:576
  242.1 0.0 copy-start
  242.1 0.0 slice-start
  242.1 6.2 %copy.29 = bf16[2,640,2048]{2,1,0:T(8,128)(2,1)} copy(bf16[2,640,2048]{2,1,0:T(8,128)(2,1)} %get-tuple-element.36) | data formatting | bytes 10485760
  248.3 0.0 copy-done
  248.3 0.0 slice-start.1
  248.3 2.4 copy.30
  250.7 0.0 slice-done
  250.7 0.0 slice-done.1
  250.7 0.0 copy-start.6
  250.7 0.0 copy-start.5
  250.7 0.0 copy-start.4
  250.7 0.0 copy-start.3
  250.7 2.6 %copy.31 = bf16[2,2048,640]{2,1,0:T(8,128)(2,1)} copy(bf16[2,2048,640]{2,1,0:T(8,128)(2,1)S(1)} %bitcast.3) | data formatting | bytes 10485760
  253.3 0.0 copy-done.6
  253.3 0.0 copy-start.2
  253.3 0.0 copy-start.1
  253.3 0.8 copy.32
  254.2 0.0 copy-done.5
  254.2 0.8 copy.33
  255.0 0.0 copy-done.4
  255.0 0.8 copy.34
  255.9 0.0 copy-done.3
  255.9 0.8 copy.35
  256.7 0.0 copy-done.2
  256.7 0.8 copy.36
  257.5 0.0 copy-done.1
  257.5 0.8 copy.37
  (1 shorter events, 0.0 us)
Async XLA Ops:
  242.1 6.2 %copy-start = (bf16[2,640,2048]{2,1,0:T(8,128)(2,1)S(1)}, bf16[2,640,2048]{2,1,0:T(8,128)(2,1)}, u32[]{:S(2)}) copy-start(bf16[2,640,2048]{2,1,0:T(8,128)(2,1)} %get-tuple-element.37) | copy-start | bytes 15728644
  242.1 8.5 %slice-start = ((s8[5242880]{0:T(1024)(128)(4,1)}), s8[4194304]{0:T(1024)(128)(4,1)S(1)}, s32[]{:S(2)}) async-start(s8[5242880]{0:T(1024)(128)(4,1)} %bitcast.2), calls=%async_computation | async-start | bytes 8388608
  248.3 2.4 slice-start.1
  250.7 2.7 %copy-start.6 = (f32[2,40,2048]{2,1,0:T(8,128)S(1)}, f32[2,40,2048]{2,1,0:T(8,128)}, u32[]{:S(2)}) copy-start(f32[2,40,2048]{2,1,0:T(8,128)} %get-tuple-element.39) | copy-start | bytes 1966084
  250.7 3.5 %copy-start.5 = (f32[2,40,2048]{2,1,0:T(8,128)S(1)}, f32[2,40,2048]{2,1,0:T(8,128)}, u32[]{:S(2)}) copy-start(f32[2,40,2048]{2,1,0:T(8,128)} %get-tuple-element.40) | copy-start | bytes 1966084
  250.7 4.3 %copy-start.4 = (f32[2,128,640]{2,1,0:T(8,128)S(1)}, f32[2,128,640]{2,1,0:T(8,128)}, u32[]{:S(2)}) copy-start(f32[2,128,640]{2,1,0:T(8,128)} %get-tuple-element.41) | copy-start | bytes 1966084
  250.7 5.2 %copy-start.3 = (f32[2,40,2048]{2,1,0:T(8,128)S(1)}, f32[2,40,2048]{2,1,0:T(8,128)}, u32[]{:S(2)}) copy-start(f32[2,40,2048]{2,1,0:T(8,128)} %get-tuple-element.42) | copy-start | bytes 1966084
  253.3 3.4 %copy-start.2 = (f32[2,40,2048]{2,1,0:T(8,128)S(1)}, f32[2,40,2048]{2,1,0:T(8,128)}, u32[]{:S(2)}) copy-start(f32[2,40,2048]{2,1,0:T(8,128)} %get-tuple-element.43) | copy-start | bytes 1966084
  253.3 4.2 %copy-start.1 = (f32[2,128,640]{2,1,0:T(8,128)S(1)}, f32[2,128,640]{2,1,0:T(8,128)}, u32[]{:S(2)}) copy-start(f32[2,128,640]{2,1,0:T(8,128)} %get-tuple-element.44) | copy-start | bytes 1966084

commit v6 on v5

--- a/solution.py
+++ b/solution.py
@@ -38,7 +38,7 @@
     act, actt, dy, dyt, wg, wu, wd, dgu, prod, own_g, got_g, own_d, got_d, slot_g, slot_d,
     wo_g, wo_d, m_g, v_g, m_d, v_d,
     load, x_load, first_out, opt_load, pair_send, pair_got, rs_start, rs_send, rs_got, ag_send, ag_got, fw_send, fw_got, keep_w, keep_m, keep_v,
-    dpair_send, dpair_got, drs_start, drs_send, drs_got, dag_send, dag_got, dfw_send, dfw_got, dkeep_w, dkeep_m, dkeep_v, credit,
+    dpair_send, dpair_got, drs_start, drs_send, drs_got, dag_send, dag_got, dfw_send, dfw_got, dkeep_w, dkeep_m, dkeep_v, credit, dcredit,
 ):
     chips = n // 2
     tokens, d = dy.shape
@@ -355,10 +355,6 @@
                     def _():
                         pltpu.make_async_copy(got_g.at[j], got_g.at[j], pair_got.at[q]).wait()
 
-                    @pl.when((o == 0) & (j == STRIPS - 1))
-                    def _():
-                        pltpu.make_async_copy(got_d, got_d, dpair_got.at[r]).wait()
-
                     @pl.when((o == far) & (g == 0))
                     def _():
                         for copy in params:
@@ -376,26 +372,46 @@
                 def _():
                     gather_step(o - far, layer, j, q, k)
 
-                @pl.when(j == STRIPS - 1)
-                def _():
-                    @pl.when(o < far)
-                    def _():
-                        dring_step(o, layer, r, k)
-
-                    @pl.when(o == far)
-                    def _():
-                        down_own_step(layer, r, k)
-
-                    @pl.when(o > far)
-                    def _():
-                        down_gather_step(o - far, layer, r, k)
-
                 if k == 1:
 
                     @pl.when((o == far) & (r < layers - 1))
                     def _():
                         pl.semaphore_signal(credit, inc=1, device_id={"dp": mate}, device_id_type=MESH)
 
+        def down_advance(lag, k):
+            g = i - lag
+            r, j = g // turns, g % turns
+            slow = r < layers - 1
+            o = jnp.where(slow, (lag - 1) * 2, (lag - 1) * per) + p // 2
+            layer = top - r
+            go = (g >= 0) & (g <= last) & (j == STRIPS - 1) & (o < steps) & (p // 2 < jnp.where(slow, 2, per))
+
+            @pl.when(go)
+            def _():
+                if k == 0:
+
+                    @pl.when(o == 0)
+                    def _():
+                        pltpu.make_async_copy(got_d, got_d, dpair_got.at[r]).wait()
+
+                @pl.when(o < far)
+                def _():
+                    dring_step(o, layer, r, k)
+
+                @pl.when(o == far)
+                def _():
+                    down_own_step(layer, r, k)
+
+                @pl.when(o > far)
+                def _():
+                    down_gather_step(o - far, layer, r, k)
+
+                if k == 1:
+
+                    @pl.when((o == far) & slow)
+                    def _():
+                        pl.semaphore_signal(dcredit, inc=1, device_id={"dp": mate}, device_id_type=MESH)
+
         for k in range(2):
 
             @pl.when(p % 2 == k)
@@ -405,6 +421,12 @@
                     return carry
 
                 lax.fori_loop(0, lags, lag_step, 0)
+
+                def down_lag_step(idx, carry):
+                    down_advance(1 + idx, k)
+                    return carry
+
+                lax.fori_loop(0, -(-steps // 2), down_lag_step, 0)
 
     def pair_copy(j, q):
         return remote(own_g.at[STRIPS + q % 2], got_g.at[j], pair_send.at[q], pair_got.at[q], mate)
@@ -474,6 +496,10 @@
 
             @pl.when(j == STRIPS - 1)
             def _():
+                @pl.when(r > 0)
+                def _():
+                    pl.semaphore_wait(dcredit, 1)
+
                 dpair_copy(r).start()
 
         @pl.when((i < last) & (j == STRIPS))
@@ -571,7 +597,7 @@
             sem((r,)), sem((r,)),
             sem((r, 2)), sem((r, 2)), sem((r, 2, chips - 1)), sem((r, 2)), sem((r, 2, chips - 1)), sem((r, 2)), sem((r, 2)),
             sem((r, 2)), sem((r, 2)), sem((r, 2)),
-            pltpu.SemaphoreType.REGULAR,
+            pltpu.SemaphoreType.REGULAR, pltpu.SemaphoreType.REGULAR,
         ]
         return pl.pallas_call(
             functools.partial(train, n),

time: 258 us -> 262 us (1.016)
  Pallas kernels: 241 us -> 245 us
    pallas_call x1, Pallas kernels: 241 us -> 245 us  [body(): pl.pallas_call(functools.partial(train, n), in_specs=[ANY] * 11, out_spec...]
where the time goes in v6:
time: 262 us
  Pallas kernels  245 us (94%)
  local copies, waits for them, and re-layouts  16.2 us (6%)
    pallas_call x1, Pallas kernels, body(): pl.pallas_call(functools.partial(train, n), in_specs=[ANY] * 11, out_spec...  245 us
    unnamed x27, local copies, waits for them, and re-layouts  16.2 us

profile of v6, /device:TPU:21, one launch (start us, length us, event | category | flops | bytes accessed | tf_op | source)
XLA Modules:
  0.0 262.2 jit_solution(14760815453996875539)
XLA Ops:
  0.6 245.3 %step.1 = (bf16[2,640,2048]{2,1,0:T(8,128)(2,1)}, bf16[2,640,2048]{2,1,0:T(8,128)(2,1)}, bf16[2,2048,640]{2,1,0:T(8,128)(2,1)}, f32[2,40,2048]{2,1,0:T(8,128)}, ...) custom-call(bf16[2048,640]{1,0:T(8,128)(2,1)} %bitcast.4, ...), custom_call_target="tpu_custom_call" | custom-call | tf_op jit(solution)/shard_map/step/pallas_call | solution.py:602
  245.9 0.0 copy-start
  245.9 0.0 slice-start
  245.9 6.2 %copy.29 = bf16[2,640,2048]{2,1,0:T(8,128)(2,1)} copy(bf16[2,640,2048]{2,1,0:T(8,128)(2,1)} %get-tuple-element.36) | data formatting | bytes 10485760
  252.1 0.0 copy-done
  252.1 0.0 slice-start.1
  252.1 2.4 copy.30
  254.5 0.0 slice-done
  254.5 0.0 slice-done.1
  254.5 0.0 copy-start.6
  254.5 0.0 copy-start.5
  254.5 0.0 copy-start.4
  254.5 0.0 copy-start.3
  254.5 2.6 %copy.31 = bf16[2,2048,640]{2,1,0:T(8,128)(2,1)} copy(bf16[2,2048,640]{2,1,0:T(8,128)(2,1)S(1)} %bitcast.3) | data formatting | bytes 10485760
  257.1 0.0 copy-done.6
  257.1 0.0 copy-start.2
  257.1 0.0 copy-start.1
  257.1 0.8 copy.32
  258.0 0.0 copy-done.5
  258.0 0.8 copy.33
  258.8 0.0 copy-done.4
  258.8 0.8 copy.34
  259.7 0.0 copy-done.3
  259.7 0.8 copy.35
  260.5 0.0 copy-done.2
  260.5 0.8 copy.36
  261.3 0.0 copy-done.1
  261.3 0.8 copy.37
  (1 shorter events, 0.0 us)
Async XLA Ops:
  245.9 6.2 %copy-start = (bf16[2,640,2048]{2,1,0:T(8,128)(2,1)S(1)}, bf16[2,640,2048]{2,1,0:T(8,128)(2,1)}, u32[]{:S(2)}) copy-start(bf16[2,640,2048]{2,1,0:T(8,128)(2,1)} %get-tuple-element.37) | copy-start | bytes 15728644
  245.9 8.5 %slice-start = ((s8[5242880]{0:T(1024)(128)(4,1)}), s8[4194304]{0:T(1024)(128)(4,1)S(1)}, s32[]{:S(2)}) async-start(s8[5242880]{0:T(1024)(128)(4,1)} %bitcast.2), calls=%async_computation | async-start | bytes 8388608
  252.1 2.4 slice-start.1
  254.5 2.7 %copy-start.6 = (f32[2,40,2048]{2,1,0:T(8,128)S(1)}, f32[2,40,2048]{2,1,0:T(8,128)}, u32[]{:S(2)}) copy-start(f32[2,40,2048]{2,1,0:T(8,128)} %get-tuple-element.39) | copy-start | bytes 1966084
  254.5 3.5 %copy-start.5 = (f32[2,40,2048]{2,1,0:T(8,128)S(1)}, f32[2,40,2048]{2,1,0:T(8,128)}, u32[]{:S(2)}) copy-start(f32[2,40,2048]{2,1,0:T(8,128)} %get-tuple-element.40) | copy-start | bytes 1966084
  254.5 4.3 %copy-start.4 = (f32[2,128,640]{2,1,0:T(8,128)S(1)}, f32[2,128,640]{2,1,0:T(8,128)}, u32[]{:S(2)}) copy-start(f32[2,128,640]{2,1,0:T(8,128)} %get-tuple-element.41) | copy-start | bytes 1966084
  254.5 5.2 %copy-start.3 = (f32[2,40,2048]{2,1,0:T(8,128)S(1)}, f32[2,40,2048]{2,1,0:T(8,128)}, u32[]{:S(2)}) copy-start(f32[2,40,2048]{2,1,0:T(8,128)} %get-tuple-element.42) | copy-start | bytes 1966084
  257.1 3.4 %copy-start.2 = (f32[2,40,2048]{2,1,0:T(8,128)S(1)}, f32[2,40,2048]{2,1,0:T(8,128)}, u32[]{:S(2)}) copy-start(f32[2,40,2048]{2,1,0:T(8,128)} %get-tuple-element.43) | copy-start | bytes 1966084
  257.1 4.2 %copy-start.1 = (f32[2,128,640]{2,1,0:T(8,128)S(1)}, f32[2,128,640]{2,1,0:T(8,128)}, u32[]{:S(2)}) copy-start(f32[2,128,640]{2,1,0:T(8,128)} %get-tuple-element.44) | copy-start | bytes 1966084

commit v7 on v5

--- a/solution.py
+++ b/solution.py
@@ -401,7 +401,7 @@
             @pl.when(p % 2 == k)
             def _():
                 def lag_step(idx, carry):
-                    advance(lags - idx, k)
+                    advance(1 + idx, k)
                     return carry
 
                 lax.fori_loop(0, lags, lag_step, 0)

time: 258 us -> 258 us (level)
  no operation moved by 1% of the time
where the time goes in v7:
time: 258 us
  Pallas kernels  241 us (93%)
  local copies, waits for them, and re-layouts  16.2 us (6%)
    pallas_call x1, Pallas kernels, body(): pl.pallas_call(functools.partial(train, n), in_specs=[ANY] * 11, out_spec...  241 us
    unnamed x27, local copies, waits for them, and re-layouts  16.2 us

profile of v7, /device:TPU:21, one launch (start us, length us, event | category | flops | bytes accessed | tf_op | source)
XLA Modules:
  0.0 257.8 jit_solution(10509915693249421684)
XLA Ops:
  0.6 240.9 %step.1 = (bf16[2,640,2048]{2,1,0:T(8,128)(2,1)}, bf16[2,640,2048]{2,1,0:T(8,128)(2,1)}, bf16[2,2048,640]{2,1,0:T(8,128)(2,1)}, f32[2,40,2048]{2,1,0:T(8,128)}, ...) custom-call(bf16[2048,640]{1,0:T(8,128)(2,1)} %bitcast.4, ...), custom_call_target="tpu_custom_call" | custom-call | tf_op jit(solution)/shard_map/step/pallas_call | solution.py:576
  241.6 0.0 copy-start
  241.6 0.0 slice-start
  241.6 6.2 %copy.29 = bf16[2,640,2048]{2,1,0:T(8,128)(2,1)} copy(bf16[2,640,2048]{2,1,0:T(8,128)(2,1)} %get-tuple-element.36) | data formatting | bytes 10485760
  247.7 0.0 copy-done
  247.7 0.0 slice-start.1
  247.7 2.4 copy.30
  250.1 0.0 slice-done
  250.1 0.0 slice-done.1
  250.1 0.0 copy-start.6
  250.1 0.0 copy-start.5
  250.1 0.0 copy-start.4
  250.1 0.0 copy-start.3
  250.1 2.6 %copy.31 = bf16[2,2048,640]{2,1,0:T(8,128)(2,1)} copy(bf16[2,2048,640]{2,1,0:T(8,128)(2,1)S(1)} %bitcast.3) | data formatting | bytes 10485760
  252.8 0.0 copy-done.6
  252.8 0.0 copy-start.2
  252.8 0.0 copy-start.1
  252.8 0.8 copy.32
  253.6 0.0 copy-done.5
  253.6 0.8 copy.33
  254.5 0.0 copy-done.4
  254.5 0.8 copy.34
  255.3 0.0 copy-done.3
  255.3 0.8 copy.35
  256.2 0.0 copy-done.2
  256.2 0.8 copy.36
  257.0 0.0 copy-done.1
  257.0 0.8 copy.37
  (1 shorter events, 0.0 us)
Async XLA Ops:
  241.6 6.2 %copy-start = (bf16[2,640,2048]{2,1,0:T(8,128)(2,1)S(1)}, bf16[2,640,2048]{2,1,0:T(8,128)(2,1)}, u32[]{:S(2)}) copy-start(bf16[2,640,2048]{2,1,0:T(8,128)(2,1)} %get-tuple-element.37) | copy-start | bytes 15728644
  241.6 8.5 %slice-start = ((s8[5242880]{0:T(1024)(128)(4,1)}), s8[4194304]{0:T(1024)(128)(4,1)S(1)}, s32[]{:S(2)}) async-start(s8[5242880]{0:T(1024)(128)(4,1)} %bitcast.2), calls=%async_computation | async-start | bytes 8388608
  247.7 2.4 slice-start.1
  250.1 2.7 %copy-start.6 = (f32[2,40,2048]{2,1,0:T(8,128)S(1)}, f32[2,40,2048]{2,1,0:T(8,128)}, u32[]{:S(2)}) copy-start(f32[2,40,2048]{2,1,0:T(8,128)} %get-tuple-element.39) | copy-start | bytes 1966084
  250.1 3.5 %copy-start.5 = (f32[2,40,2048]{2,1,0:T(8,128)S(1)}, f32[2,40,2048]{2,1,0:T(8,128)}, u32[]{:S(2)}) copy-start(f32[2,40,2048]{2,1,0:T(8,128)} %get-tuple-element.40) | copy-start | bytes 1966084
  250.1 4.3 %copy-start.4 = (f32[2,128,640]{2,1,0:T(8,128)S(1)}, f32[2,128,640]{2,1,0:T(8,128)}, u32[]{:S(2)}) copy-start(f32[2,128,640]{2,1,0:T(8,128)} %get-tuple-element.41) | copy-start | bytes 1966084
  250.1 5.2 %copy-start.3 = (f32[2,40,2048]{2,1,0:T(8,128)S(1)}, f32[2,40,2048]{2,1,0:T(8,128)}, u32[]{:S(2)}) copy-start(f32[2,40,2048]{2,1,0:T(8,128)} %get-tuple-element.42) | copy-start | bytes 1966084
  252.8 3.4 %copy-start.2 = (f32[2,40,2048]{2,1,0:T(8,128)S(1)}, f32[2,40,2048]{2,1,0:T(8,128)}, u32[]{:S(2)}) copy-start(f32[2,40,2048]{2,1,0:T(8,128)} %get-tuple-element.43) | copy-start | bytes 1966084
  252.8 4.2 %copy-start.1 = (f32[2,128,640]{2,1,0:T(8,128)S(1)}, f32[2,128,640]{2,1,0:T(8,128)}, u32[]{:S(2)}) copy-start(f32[2,128,640]{2,1,0:T(8,128)} %get-tuple-element.44) | copy-start | bytes 1966084
